TPU v7x, 128 devices: a whole 4x4x4 slice. The times are simulated.
128 devices in a mesh: expert: 4 (over z), shard: 32 (over y, x, core).
Axes of the slice: x: 4, y: 4, z: 4, core: 2. Of those that a mesh axis runs over, the one named last changes fastest.
Arguments:
- tokens: bfloat16 [3072, 4096], P(('expert', 'shard')), may hold values from -0.19921875 to 0.19921875
- expert_ids: int32 [3072, 2], P(('expert', 'shard')), may hold values from 0 to 3, all different within a row; in each aligned block of 24 rows (0 to 23, 24 to 47, ...) at most 16 rows name the same one
- weight_gate: bfloat16 [4, 4096, 8192], P('expert', None, 'shard'), may hold values from -0.09375 to 0.09375
- weight_up: bfloat16 [4, 4096, 8192], P('expert', None, 'shard'), may hold values from -0.09375 to 0.09375
- gate_pre: bfloat16 [4, 2048, 8192], P('expert', None, 'shard'), may hold values from -8 to 8
- up_pre: bfloat16 [4, 2048, 8192], P('expert', None, 'shard'), may hold values from -6 to 6
- hidden_grad: bfloat16 [4, 2048, 8192], P('expert', None, 'shard'), may hold values from -6 to 6
Outputs:
- token_grad: bfloat16 [3072, 4096], P(('expert', 'shard'))
- gate_weight_grad: float32 [4, 4096, 8192], P('expert', None, 'shard')
- up_weight_grad: float32 [4, 4096, 8192], P('expert', None, 'shard')
Inputs may be any that keep to these rules, and one draw needn't show every extreme that they name: `expert_ids`: each token names 2 different experts. Among the tokens of one device no expert is named more than 16 times, and in every draw some device names some expert exactly 16 times.
All inputs are finite; a program needn't handle non-finite values.
Results may differ from a plain program's by a relative error of at most 0.02.
Values may be sent and summed in bfloat16 or wider, within the bound.
A program may use at most 192 MiB of HBM per device.

v0:
```python
import jax
import jax.numpy as jnp
from jax import lax
from jax.sharding import Mesh
from jax.sharding import PartitionSpec as P

SHARD = ("shard_0", "shard_1", "shard_2")
EXPERT_SHARD = ("expert", "shard_0", "shard_1", "shard_2")


def joined_along(tiles, dim):
    lengths = list(tiles.shape[1:])
    lengths[dim] *= tiles.shape[0]
    return jnp.moveaxis(tiles, 0, dim).reshape(lengths)


def all_blocks(array, axes, sequence):
    tiles = array
    for k in sequence:
        tiles = lax.all_gather(tiles, axes[k])
    done = sequence[::-1]
    back = [done.index(k) for k in range(len(axes))]
    tiles = tiles.transpose(*back, *range(len(axes), tiles.ndim))
    return tiles.reshape(-1, *array.shape)


def whole_of(array, axes, sequence, dim):
    return joined_along(all_blocks(array, axes, sequence), dim)


def split_up(array, dim, peers):
    before, after = (array.shape[:dim], array.shape[dim + 1 :])
    return jnp.moveaxis(array.reshape(*before, peers, -1, *after), dim, 0)


def scatter_pairs(array, chips, core, dim):
    sizes = (lax.axis_size(chips), lax.axis_size(core))
    tiles = split_up(array, dim, sizes[0] * sizes[1])
    inside = tiles.shape[1:]
    tiles = tiles.reshape(*sizes, *inside).swapaxes(0, 1).reshape(-1, *inside)
    tiles = lax.psum_scatter(tiles, core, scatter_dimension=0, tiled=True)
    return lax.psum_scatter(tiles, chips, scatter_dimension=0, tiled=True)[0]


def swiglu_grads(gate_values, up_values, hidden_cotangent):
    gate_float = gate_values.astype(jnp.float32)
    up_float = up_values.astype(jnp.float32)
    cotangent = hidden_cotangent.astype(jnp.float32)
    sigmoid_gate = jax.nn.sigmoid(gate_float)
    gate_grad = (
        cotangent * up_float * sigmoid_gate * (1.0 + gate_float * (1.0 - sigmoid_gate))
    ).astype(jnp.bfloat16)
    up_grad = (cotangent * gate_float * sigmoid_gate).astype(jnp.bfloat16)
    return (gate_grad, up_grad)


def slot_table(expert_ids, groups, capacity):
    token_count = expert_ids.shape[0]
    choices_per = expert_ids.shape[1]
    labels = lax.broadcasted_iota(jnp.int32, (1, 1, groups), 2)
    one_hot = (expert_ids[:, :, None] == labels).astype(jnp.int32)
    flat_hits = one_hot.reshape(token_count * choices_per, groups)
    earlier = jnp.cumsum(flat_hits, axis=0) - flat_hits
    slot_index = jnp.sum(flat_hits * earlier, axis=1).reshape(token_count, choices_per)
    slot_labels = lax.broadcasted_iota(jnp.int32, (1, 1, 1, capacity), 3)
    slot_hits = one_hot[:, :, :, None] * (slot_index[:, :, None, None] == slot_labels).astype(
        jnp.int32
    )
    selection = jnp.sum(slot_hits, axis=1).reshape(token_count, groups * capacity)
    return selection.astype(jnp.bfloat16)


def rows_inner(left_rows, right_rows):
    return lax.dot_general(
        left_rows, right_rows, (((0,), (0,)), ((), ())), preferred_element_type=jnp.float32
    )


def times_transposed(left_rows, weights):
    return lax.dot_general(
        left_rows, weights, (((1,), (1,)), ((), ())), preferred_element_type=jnp.float32
    )


def on_device(tokens, expert_ids, weight_gate, weight_up, gate_pre, up_pre, hidden_grad):
    groups = lax.axis_size("expert")
    shards = lax.axis_size(SHARD)
    model_width = tokens.shape[1]
    capacity = gate_pre.shape[1] // (groups * shards)
    selection = slot_table(expert_ids, groups, capacity)
    outgoing = rows_inner(selection, tokens).astype(jnp.bfloat16)
    gate_grad, up_grad = swiglu_grads(gate_pre[0], up_pre[0], hidden_grad[0])
    gate_matrix = weight_gate[0]
    up_matrix = weight_up[0]
    arrived = lax.all_to_all(
        outgoing.reshape(groups, capacity, model_width),
        "expert",
        split_axis=0,
        concat_axis=0,
        tiled=True,
    )
    block_rows = whole_of(
        arrived.reshape(groups * capacity, model_width),
        (("shard_0", "shard_1"), "shard_2"),
        (0, 1),
        0,
    )
    gate_rows = gate_grad
    up_rows = up_grad
    gate_wgrad = rows_inner(block_rows, gate_rows)
    up_wgrad = rows_inner(block_rows, up_rows)
    gate_rows = gate_grad
    up_rows = up_grad
    summed = scatter_pairs(
        (times_transposed(gate_rows, gate_matrix) + times_transposed(up_rows, up_matrix)).astype(
            jnp.bfloat16
        ),
        ("shard_0", "shard_1"),
        "shard_2",
        0,
    ).astype(jnp.float32)
    outbound = summed.astype(jnp.bfloat16).reshape(groups, capacity, model_width)
    returned = lax.all_to_all(outbound, "expert", split_axis=0, concat_axis=0, tiled=True)
    returned = returned.reshape(groups * capacity, model_width)
    token_grad = times_transposed(selection, returned.T).astype(jnp.bfloat16)
    return (token_grad, gate_wgrad[None], up_wgrad[None])


def solution(mesh):
    torus = Mesh(
        mesh.devices.reshape(mesh.shape["expert"], 4, 4, 2),
        ("expert", "shard_0", "shard_1", "shard_2"),
    )
    placed = (
        P(EXPERT_SHARD, None),
        P(EXPERT_SHARD, None),
        P("expert", None, SHARD),
        P("expert", None, SHARD),
        P("expert", None, SHARD),
        P("expert", None, SHARD),
        P("expert", None, SHARD),
    )
    return jax.shard_map(
        on_device,
        mesh=torus,
        in_specs=placed,
        out_specs=(P(EXPERT_SHARD, None), P("expert", None, SHARD), P("expert", None, SHARD)),
        check_vma=False,
    )
```

profile of v0, /device:TPU:1, one launch (start us, length us, event | category | flops | bytes accessed | tf_op | source)
XLA Modules:
  0.0 217.6 jit_solution(4858613945557598756)
XLA Ops:
  8.0 0.0 copy-start
  8.0 0.0 all-gather.4.cloned.1.call-start
  8.1 0.9 copy.23
  9.0 0.7 fusion.19
  9.7 0.1 eq.49
  9.8 0.1 fusion.17
  9.8 0.1 reduce_window_sum.11
  9.9 0.2 select_reduce_fusion
  10.1 0.1 eq.53
  10.2 0.1 copy.24
  10.3 1.2 convolution_convert_fusion
  11.5 14.4 %all_to_all.10 = bf16[4,16,4096]{2,1,0:T(8,128)(2,1)} all-to-all(bf16[4,16,4096]{2,1,0:T(8,128)(2,1)S(1)} %bitcast.49), channel_id=1, replica_groups=mesh['expert'=4,'shard_0'=4,'shard_1'=4,'shard_2'=2] {'expert'}, dimensions={0} | all-to-all | bytes 1048576 | tf_op jit(solution)/shard_map/all_to_all | solution.py:95
  25.9 0.0 all-gather.4.cloned.1.call-update
  25.9 0.0 reduce-scatter.5.cloned.1.call-start
  26.0 15.6 %fusion.11 = f32[2048,4096]{1,0:T(8,128)} fusion(bf16[1,4096,256]{2,1,0:T(8,128)(2,1)S(1)} %copy-done, bf16[1,2048,256]{2,1,0:T(8,128)(2,1)S(1)} %copy-done.3, bf16[1,2048,256]{2,1,0:T(8,128)(2,1)} %param.11, bf16[1,2048,256]{2,1,0:T(8,128)(2,1)} %param.12), kind=kOutput, calls=%fused_computation.20 | convolution fusion | flops 4301783040 | bytes 38797312 | tf_op jit(solution)/shard_map/dot_general | solution.py:80
  41.6 20.2 %add_convert_fusion = bf16[2048,4096]{1,0:T(8,128)(2,1)} fusion(f32[2048,4096]{1,0:T(8,128)} %fusion.11, bf16[1,4096,256]{2,1,0:T(8,128)(2,1)} %param.10, bf16[1,2048,256]{2,1,0:T(8,128)(2,1)} %param.11, bf16[1,2048,256]{2,1,0:T(8,128)(2,1)S(1)} %copy-done.3), kind=kOutput, calls=%fused_computation | convolution fusion | flops 4315938816 | bytes 54525952 | tf_op jit(solution)/shard_map/dot_general | solution.py:80
  61.8 14.1 %copy.25 = bf16[16,2,64,4096]{3,2,0,1:T(8,128)(2,1)} copy(bf16[16,2,64,4096]{3,2,1,0:T(8,128)(2,1)} %bitcast.43) | data formatting | bytes 33554432 | tf_op jit(solution)/shard_map/reshape;reshape | solution.py:40
  75.9 0.0 reduce-scatter.5.cloned.1.call-update
  75.9 0.0 all-gather.6.cloned.1.call-start
  76.0 21.2 %all-gather.4.cloned.1.call-done = bf16[16,64,4096]{2,1,0:T(8,128)(2,1)} async-done(((bf16[1,64,4096]{2,1,0:T(8,128)(2,1)}), bf16[16,64,4096]{2,1,0:T(8,128)(2,1)}) %all-gather.4.cloned.1.call-update) | async-done | bytes 8388624 | tf_op jit(solution)/shard_map/all_gather | solution.py:20
  97.2 0.0 all-gather.6.cloned.1.call-update
  97.3 0.0 reduce-scatter.7.cloned.1.call-start
  97.3 7.8 %reduce-scatter.5.cloned.1.call-done = bf16[16,64,4096]{2,1,0:T(8,128)(2,1)} async-done(((bf16[32,64,4096]{2,1,0:T(8,128)(2,1)}), bf16[16,64,4096]{2,1,0:T(8,128)(2,1)}) %reduce-scatter.5.cloned.1.call-update) | async-done | bytes 8388624 | tf_op jit(solution)/shard_map/reduce_scatter | solution.py:41
  105.1 0.0 reduce-scatter.7.cloned.1.call-update
  105.2 35.5 %all-gather.6.cloned.1.call-done = bf16[32,64,4096]{2,1,0:T(8,128)(2,1)} async-done(((bf16[16,64,4096]{2,1,0:T(8,128)(2,1)}), bf16[32,64,4096]{2,1,0:T(8,128)(2,1)}) %all-gather.6.cloned.1.call-update) | async-done | bytes 16777232 | tf_op jit(solution)/shard_map/all_gather | solution.py:20
  140.6 8.8 %copy.26 = bf16[16,2,64,4096]{3,2,1,0:T(8,128)(2,1)S(1)} copy(bf16[16,2,64,4096]{3,2,0,1:T(8,128)(2,1)} %bitcast.45) | data formatting | bytes 33554432 | tf_op jit(solution)/shard_map/transpose | solution.py:23
  149.5 6.1 %copy-done.2 = bf16[16,2,64,4096]{3,2,1,0:T(8,128)(2,1)} copy-done((bf16[16,2,64,4096]{3,2,1,0:T(8,128)(2,1)}, bf16[16,2,64,4096]{3,2,1,0:T(8,128)(2,1)S(1)}, u32[]{:S(2)}) %copy-start.2) | copy-done | bytes 16777240
  155.6 6.7 %convolution_bitcast_fusion.1 = f32[1,4096,256]{2,1,0:T(8,128)} fusion(bf16[2048,4096]{1,0:T(8,128)(2,1)S(1)} %bitcast.46, bf16[1,2048,256]{2,1,0:T(8,128)(2,1)S(1)} %copy-done.3, bf16[1,2048,256]{2,1,0:T(8,128)(2,1)S(1)} %copy-done.4, bf16[1,2048,256]{2,1,0:T(8,128)(2,1)S(1)} %copy-done.5), kind=kOutput, calls=%fused_computation.2 | convolution fusion | flops 4301783040 | bytes 24117248 | tf_op jit(solution)/shard_map/dot_general | solution.py:74
  162.3 28.2 %reduce-scatter.7.cloned.1.call-done = bf16[1,64,4096]{2,1,0:T(8,128)(2,1)} async-done(((bf16[16,64,4096]{2,1,0:T(8,128)(2,1)}), bf16[1,64,4096]{2,1,0:T(8,128)(2,1)}) %reduce-scatter.7.cloned.1.call-update) | async-done | bytes 524304
  190.6 4.3 %all-to-all-start = ((bf16[4,16,4096]{2,1,0:T(8,128)(2,1)}), bf16[4,16,4096]{2,1,0:T(8,128)(2,1)}, u32[]{:S(2)}, u32[]{:S(2)}) async-start(bf16[4,16,4096]{2,1,0:T(8,128)(2,1)} %bitcast.50), calls=%async_computation.1 | async-start | bytes 1048576 | tf_op jit(solution)/shard_map/all_to_all | solution.py:123
  194.9 13.3 %convolution_bitcast_fusion = f32[1,4096,256]{2,1,0:T(8,128)} fusion(bf16[2048,4096]{1,0:T(8,128)(2,1)} %bitcast.47, bf16[1,2048,256]{2,1,0:T(8,128)(2,1)} %param.11, bf16[1,2048,256]{2,1,0:T(8,128)(2,1)S(1)} %copy-done.3), kind=kOutput, calls=%fused_computation.1 | convolution fusion | flops 4299161600 | bytes 23068672 | tf_op jit(solution)/shard_map/dot_general | solution.py:74
  208.2 2.0 fusion
  (14 shorter events, 0.1 us)
Async XLA Ops:
  8.0 18.0 %copy-start = (bf16[1,4096,256]{2,1,0:T(8,128)(2,1)S(1)}, bf16[1,4096,256]{2,1,0:T(8,128)(2,1)}, u32[]{:S(2)}) copy-start(bf16[1,4096,256]{2,1,0:T(8,128)(2,1)} %param.9) | copy-start | bytes 6291460
  8.0 18.0 %copy-start.3 = (bf16[1,2048,256]{2,1,0:T(8,128)(2,1)S(1)}, bf16[1,2048,256]{2,1,0:T(8,128)(2,1)}, u32[]{:S(2)}) copy-start(bf16[1,2048,256]{2,1,0:T(8,128)(2,1)} %param.13) | copy-start | bytes 3145732
  8.0 89.2 %all-gather.4.cloned.1.call-start = ((), (), s32[]{:S(2)}) async-start(), calls=%async_computation.5 | async-start | bytes 8912896 | tf_op jit(solution)/shard_map/all_gather | solution.py:20
  25.9 79.2 %reduce-scatter.5.cloned.1.call-start = ((), (), s32[]{:S(2)}) async-start(), calls=%async_computation.4 | async-start | bytes 25165824 | tf_op jit(solution)/shard_map/reduce_scatter | solution.py:41
  75.9 64.7 %all-gather.6.cloned.1.call-start = ((), (), s32[]{:S(2)}) async-start(), calls=%async_computation.6 | async-start | bytes 25165824 | tf_op jit(solution)/shard_map/all_gather | solution.py:20
  97.3 93.3 %reduce-scatter.7.cloned.1.call-start = ((), (), s32[]{:S(2)}) async-start(), calls=%async_computation.7 | async-start | bytes 8912896
  140.6 15.0 %copy-start.4 = (bf16[1,2048,256]{2,1,0:T(8,128)(2,1)S(1)}, bf16[1,2048,256]{2,1,0:T(8,128)(2,1)}, u32[]{:S(2)}) copy-start(bf16[1,2048,256]{2,1,0:T(8,128)(2,1)} %param.11) | copy-start | bytes 3145732
  140.6 15.0 %copy-start.5 = (bf16[1,2048,256]{2,1,0:T(8,128)(2,1)S(1)}, bf16[1,2048,256]{2,1,0:T(8,128)(2,1)}, u32[]{:S(2)}) copy-start(bf16[1,2048,256]{2,1,0:T(8,128)(2,1)} %param.12) | copy-start | bytes 3145732
  149.5 6.1 %copy-start.2 = (bf16[16,2,64,4096]{3,2,1,0:T(8,128)(2,1)}, bf16[16,2,64,4096]{3,2,1,0:T(8,128)(2,1)S(1)}, u32[]{:S(2)}) copy-start(bf16[16,2,64,4096]{3,2,1,0:T(8,128)(2,1)S(1)} %copy.26) | copy-start | bytes 50331652
  190.6 17.6 %all-to-all-start = ((bf16[4,16,4096]{2,1,0:T(8,128)(2,1)}), bf16[4,16,4096]{2,1,0:T(8,128)(2,1)}, u32[]{:S(2)}, u32[]{:S(2)}) async-start(bf16[4,16,4096]{2,1,0:T(8,128)(2,1)} %bitcast.50), calls=%async_computation.1 | async-start | bytes 1048576 | tf_op jit(solution)/shard_map/all_to_all | solution.py:123
  194.9 15.3 %copy-start.1 = (bf16[1,4096,256]{2,1,0:T(8,128)(2,1)S(1)}, bf16[1,4096,256]{2,1,0:T(8,128)(2,1)}, u32[]{:S(2)}) copy-start(bf16[1,4096,256]{2,1,0:T(8,128)(2,1)} %param.9) | copy-start | bytes 6291460
Sparse Core Ops, SparseCore 0:
  26.1 71.1 all-gather.3
  105.3 85.2 reduce-scatter.6
Sparse Core Ops, SparseCore 1:
  76.0 29.0 reduce-scatter.4
  106.7 33.9 all-gather.5
where the time goes:
time: 219 us; the launch traced here: 218 us
  waiting for transfers between devices  92.8 us (42%)
  matrix products  59 us (27%)
  local copies, waits for them, and re-layouts  30.3 us (14%)
  between operations  15.6 us (7%)
  blocking collectives  14.4 us (7%)
  starting transfers between devices  4.48 us (2%)
    all_gather x2, waiting for transfers between devices, all_blocks(): tiles = lax.all_gather(tiles, axes[k])  56.7 us
    dot_general x3, matrix products, times_transposed(): lax.dot_general(left_rows, weights, (((1,), (1,)), ((), ())), preferred_e...  37.7 us
    unnamed x5, waiting for transfers between devices  28.3 us
    dot_general x3, matrix products, rows_inner(): lax.dot_general(left_rows, right_rows, (((0,), (0,)), ((), ())), preferre...  21.3 us
    all_to_all x1, blocking collectives, on_device(): lax.all_to_all(outgoing.reshape(groups, capacity, model_width), 'expert',...  14.4 us
    another operation x1, local copies, waits for them, and re-layouts, scatter_pairs(): tiles = tiles.reshape(*sizes, *inside).swapaxes(0, 1).reshape(-1, *inside)  14.1 us
    transpose x1, local copies, waits for them, and re-layouts, all_blocks(): tiles = tiles.transpose(*back, *range(len(axes), tiles.ndim))  8.84 us
    reduce_scatter x1, waiting for transfers between devices, scatter_pairs(): tiles = lax.psum_scatter(tiles, core, scatter_dimension=0, tiled=True)  7.82 us
  transfers between devices with their start and end apart: 5, of which 4 were waited for; matrix products, arithmetic and copies ran while one was open for 36% of the time, Pallas kernels for 0%

commit v1 on v0

v1 whole, which is shorter than its diff:
```python
import functools

import jax
import jax.numpy as jnp
from jax import lax
from jax.experimental import pallas as pl
from jax.experimental.pallas import tpu as pltpu
from jax.sharding import Mesh
from jax.sharding import PartitionSpec as P

SHARD = ("shard_0", "shard_1", "shard_2")
EXPERT_SHARD = ("expert", "shard_0", "shard_1", "shard_2")
SIGN = (1, -1)
F32 = jnp.float32
BF16 = jnp.bfloat16


def shifted(value, by, size):
    return lax.rem(value + by % size, size)


def kernel(
    ids_ref, ids_t_ref, tok_ref, wg_ref, wu_ref, gate_ref, up_ref, hid_ref,
    tg_ref, og_ref, ou_ref,
    rows, grads, weights, terms, near1, far1, near2, far2, staged, pre, outgoing, returned,
    send_sem, recv_sem, local_sem, out_sem, out_send, out_recv,
):
    z = lax.axis_index("expert")
    y = lax.axis_index("shard_0")
    x = lax.axis_index("shard_1")
    c = lax.axis_index("shard_2")
    other = 1 - c
    here = y * 4 + x
    half = tok_ref.shape[1] // 2
    quarter = half // 2
    units = gate_ref.shape[2]
    tokens = tok_ref.shape[0]
    cap = 16
    part_rows = rows.shape[2] // 2

    numbers = {}

    def number(key):
        return numbers.setdefault(key, len(numbers))

    def remote(key, src, dst, device):
        i = number(key)
        return pltpu.make_async_remote_copy(
            src_ref=src,
            dst_ref=dst,
            send_sem=send_sem.at[i],
            recv_sem=recv_sem.at[i],
            device_id=device,
            device_id_type=pl.DeviceIdType.MESH,
        )

    def along(h):
        return (x, y) if h == 0 else (y, x)

    def block(h, alpha, beta):
        return beta * 4 + alpha if h == 0 else alpha * 4 + beta

    def first(h, s):
        return {"shard_1": shifted(x, SIGN[s], 4)} if h == 0 else {"shard_0": shifted(y, SIGN[s], 4)}

    def second(h, s):
        return first(1 - h, s)

    def part(p):
        return pl.ds(p * part_rows, part_rows)

    def gather1(h, s, t, arriving=False):
        alpha, beta = along(h)
        back = (1 if t == "w" else 0) + (1 if arriving else 0)
        p = 1 - s if t == "o" else s
        ref = rows.at[h, block(h, shifted(alpha, -SIGN[s] * back, 4), beta), part(p)]
        return remote(("a1", h, s, t), ref, ref, first(h, s))

    def gather2(h, s, k, t, arriving=False):
        alpha, beta = along(h)
        back = (1 if t == "w" else 0) + (1 if arriving else 0)
        p = 1 - s if t == "o" else s
        ref = rows.at[
            h, block(h, shifted(alpha, k, 4), shifted(beta, -SIGN[s] * back, 4)), part(p)
        ]
        return remote(("a2", h, s, k, t), ref, ref, second(h, s))

    def reduce1(h, s, k, t):
        alpha, beta = along(h)
        a = shifted(alpha, k, 4)
        if t == "f":
            src = terms.at[h, block(h, a, shifted(beta, 2, 4)), part(s)]
            dst = far1.at[h, s, k]
        else:
            p = 1 - s if t == "o" else s
            src = terms.at[h, block(h, a, shifted(beta, SIGN[s], 4)), part(p)]
            dst = near1.at[h, s, k, part(p)]
        return remote(("r1", h, s, k, t), src, dst, second(h, s))

    def reduce2(h, s, t):
        alpha, beta = along(h)
        if t == "f":
            src = terms.at[h, block(h, shifted(alpha, 2, 4), beta), part(s)]
            dst = far2.at[h, s]
        else:
            p = 1 - s if t == "o" else s
            src = terms.at[h, block(h, shifted(alpha, SIGN[s], 4), beta), part(p)]
            dst = near2.at[h, s, part(p)]
        return remote(("r2", h, s, t), src, dst, first(h, s))

    def slots_of(device, core):
        return pl.ds(pl.multiple_of(core * 64 + device * cap, cap), cap)

    def spread(dz, dc):
        e = shifted(z, dz, 4)
        core = shifted(c, dc, 2)
        return remote(
            ("zi", dz, dc),
            outgoing.at[core, :, pl.ds(pl.multiple_of(e * cap, cap), cap), :],
            rows.at[:, here, slots_of(z, c), :],
            {"expert": e, "shard_2": core},
        )

    def bring(dz, dc):
        j = shifted(z, dz, 4)
        core = shifted(c, dc, 2)
        return remote(
            ("zo", dz, dc),
            terms.at[:, here, slots_of(j, core), :],
            returned.at[c, :, pl.ds(pl.multiple_of(z * cap, cap), cap), :],
            {"expert": j, "shard_2": core},
        )

    partner = {"shard_2": other}

    def weight_out(which):
        ref = (wg_ref, wu_ref)[which]
        return remote(
            ("w", which),
            ref.at[0, pl.ds(pl.multiple_of(other * half, half), half), :],
            weights.at[:, pl.ds(2 * units + which * units, units)],
            partner,
        )

    def weight_in(which):
        ref = (wg_ref, wu_ref)[which]
        return pltpu.make_async_copy(
            ref.at[0, pl.ds(pl.multiple_of(c * half, half), half), :],
            weights.at[:, pl.ds(which * units, units)],
            local_sem.at[which],
        )

    def pre_in(which):
        ref = (gate_ref, up_ref, hid_ref)[which]
        return pltpu.make_async_copy(ref.at[0], pre.at[which], local_sem.at[2 + which])

    def grads_out():
        return remote(
            ("g",), grads.at[:, pl.ds(0, 2 * units)], grads.at[:, pl.ds(2 * units, 2 * units)], partner
        )

    own_in = pltpu.make_async_copy(
        outgoing.at[c, :, pl.ds(pl.multiple_of(z * cap, cap), cap), :],
        rows.at[:, here, slots_of(z, c), :],
        local_sem.at[5],
    )

    own_out = pltpu.make_async_copy(
        terms.at[:, here, slots_of(z, c), :],
        returned.at[c, :, pl.ds(pl.multiple_of(z * cap, cap), cap), :],
        local_sem.at[6],
    )

    peers = [(dz, dc) for dz in (2, 1, 3, 0) for dc in (0, 1) if (dz, dc) != (0, 0)]
    both = [(h, s) for h in (0, 1) for s in (0, 1)]

    for which in range(3):
        pre_in(which).start()
    for which in range(2):
        weight_in(which).start()
    barrier = pltpu.get_barrier_semaphore()
    for dz, dc in peers:
        pl.semaphore_signal(
            barrier, inc=1,
            device_id={"expert": shifted(z, dz, 4), "shard_2": shifted(c, dc, 2)},
            device_id_type=pl.DeviceIdType.MESH,
        )
    for h, s in both:
        pl.semaphore_signal(
            barrier, inc=1, device_id=first(h, s), device_id_type=pl.DeviceIdType.MESH
        )

    slots = 4 * cap
    expert_r = lax.broadcasted_iota(jnp.int32, (slots, tokens), 0)
    named_t = (ids_t_ref[0:1, :] == expert_r // cap) | (ids_t_ref[1:2, :] == expert_r // cap)
    before_t = (
        lax.broadcasted_iota(jnp.int32, (tokens, tokens), 0)
        < lax.broadcasted_iota(jnp.int32, (tokens, tokens), 1)
    )
    slot_t = jnp.dot(
        named_t.astype(F32).astype(BF16), before_t.astype(F32).astype(BF16),
        preferred_element_type=F32,
    )
    pick_t = jnp.where(
        named_t & (slot_t == (expert_r % cap).astype(F32)), 1.0, 0.0
    ).astype(BF16)
    for core in range(2):
        for h in range(2):
            at = core * half + h * quarter
            outgoing[core, h] = jnp.dot(
                pick_t, tok_ref[:, at:at + quarter], preferred_element_type=F32
            ).astype(BF16)

    pl.semaphore_wait(barrier, len(peers) + len(both))
    for dz, dc in peers:
        spread(dz, dc).start()
    own_in.start()
    for which in range(2):
        weight_out(which).start()

    for which in range(3):
        pre_in(which).wait()

    @pl.loop(0, pre.shape[1] // 64)
    def _(i):
        at = pl.ds(pl.multiple_of(i * 64, 64), 64)
        a = pre[0, at, :].astype(F32)
        b = pre[1, at, :].astype(F32)
        g = pre[2, at, :].astype(F32)
        sig = 1.0 / (1.0 + jnp.exp(-a))
        gs = g * sig
        grads[at, 0:units] = (gs * b * (1.0 + a * (1.0 - sig))).astype(BF16)
        grads[at, units:2 * units] = (gs * a).astype(BF16)

    grads_out().start()

    own_in.wait()
    for dz, dc in peers:
        spread(dz, dc).wait_recv()
    for t in ("f", "o"):
        for h, s in both:
            gather1(h, s, t).start()
    for t in ("f", "o"):
        for h, s in both:
            gather2(h, s, 0, t).start()

    def send_part(h, k, p):
        for s in ((0, 1) if p == 0 else (1, 0)):
            gather2(h, s, k, "f" if s == p else "o").start()

    def gather_stage(i):
        if i == 1:
            for h, s in both:
                gather1(h, s, "f", True).wait_recv()
                gather1(h, s, "w").start()
            for h in (0, 1):
                send_part(h, 3, 0)
                send_part(h, 1, 1)
        if i == 2:
            for h, s in both:
                gather1(h, s, "o", True).wait_recv()
            for h in (0, 1):
                send_part(h, 3, 1)
                send_part(h, 1, 0)
        if i == 3:
            for h, s in both:
                gather2(h, s, 0, "f", True).wait_recv()
                gather2(h, s, 0, "w").start()
        if i == 4:
            for h, s in both:
                gather1(h, s, "w", True).wait_recv()
            for h in (0, 1):
                gather2(h, 0, 2, "f").start()
                gather2(h, 1, 2, "f").start()
                gather2(h, 0, 2, "o").start()
                gather2(h, 1, 2, "o").start()
        if i == 5:
            for h in (0, 1):
                for s, k in ((0, 3), (1, 1)):
                    gather2(h, s, k, "f", True).wait_recv()
                    gather2(h, s, k, "w").start()
        if i == 6:
            for h in (0, 1):
                for s, k in ((0, 1), (1, 3)):
                    gather2(h, s, k, "f", True).wait_recv()
                    gather2(h, s, k, "w").start()

    for which in range(2):
        weight_in(which).wait()
        weight_out(which).wait_recv()
    grads_out().wait_recv()

    group = 4 * rows.shape[2]

    @pl.loop(0, 8)
    def _(i):
        for stage in range(1, 7):
            @pl.when(i == stage)
            def _():
                gather_stage(stage)
        h = i // 4
        g = i % 4

        @pl.loop(0, quarter // 256)
        def _(n):
            left = grads[pl.ds(pl.multiple_of(g * group, group), group), :]
            right = weights[pl.ds(pl.multiple_of(h * quarter + n * 256, 256), 256), :]
            out = lax.dot_general(
                left, right, (((1,), (1,)), ((), ())), preferred_element_type=F32
            ).astype(BF16)
            terms[h, pl.ds(g * 4, 4), :, pl.ds(pl.multiple_of(n * 256, 256), 256)] = out.reshape(
                4, rows.shape[2], 256
            )

    for h, s in both:
        gather2(h, s, 2, "f", True).wait_recv()
        gather2(h, s, 2, "w").start()

    for k, t in ((2, "f"), (1, "f"), (2, "o"), (3, "f")):
        for h, s in both:
            reduce1(h, s, k, t).start()

    for h, s in both:
        for k in (0, 1, 3, 2):
            gather2(h, s, k, "o", True).wait_recv()
            gather2(h, s, k, "w", True).wait_recv()

    def add_into(h, at, p, sources):
        @pl.loop(0, part_rows // 16)
        def _(i):
            lines = pl.ds(pl.multiple_of(p * part_rows + i * 16, 16), 16)
            total = terms[h, at, lines, :].astype(F32)
            for ref, base in sources:
                total = total + ref[
                    pl.ds(pl.multiple_of(base + i * 16, 16), 16), :
                ].astype(F32)
            terms[h, at, lines, :] = total.astype(BF16)

    def relay1(k):
        for h, s in both:
            reduce1(h, s, k, "f").wait_recv()
            alpha, beta = along(h)
            add_into(
                h, block(h, shifted(alpha, k, 4), shifted(beta, SIGN[s], 4)), s,
                [(far1.at[h, s, k], 0)],
            )
            reduce1(h, s, k, "w").start()

    def finish1(k):
        for h in (0, 1):
            for s in (0, 1):
                reduce1(h, s, k, "o").wait_recv()
                reduce1(h, s, k, "w").wait_recv()
            alpha, beta = along(h)
            for p in (0, 1):
                base = p * part_rows
                add_into(
                    h, block(h, shifted(alpha, k, 4), beta), p,
                    [(near1.at[h, 0, k], base), (near1.at[h, 1, k], base)],
                )

    def send1(k, t):
        for h, s in both:
            reduce1(h, s, k, t).start()

    def reduce_stage(i):
        if i == 1:
            relay1(2)
            send1(1, "o")
        if i == 2:
            relay1(1)
            send1(3, "o")
        if i == 3:
            relay1(3)
            send1(0, "f")
        if i == 4:
            finish1(2)
            for h, s in both:
                reduce2(h, s, "f").start()
            send1(0, "o")

    def out_rows(i):
        at = pl.multiple_of(c * half + i * 256, 256)
        return pl.ds(at, 256)

    def out_local(i, which):
        return pltpu.make_async_copy(
            staged.at[i, which], (og_ref, ou_ref)[which].at[0, out_rows(i), :], out_sem.at[i, which]
        )

    def out_remote(i, which):
        return pltpu.make_async_remote_copy(
            src_ref=staged.at[i, 2 + which],
            dst_ref=(og_ref, ou_ref)[which].at[0, out_rows(i), :],
            send_sem=out_send.at[i, which],
            recv_sem=out_recv.at[i, which],
            device_id=partner,
            device_id_type=pl.DeviceIdType.MESH,
        )

    all_rows = rows.shape[1] * rows.shape[2]

    @pl.loop(0, 8)
    def _(i):
        for stage in range(1, 5):
            @pl.when(i == stage)
            def _():
                reduce_stage(stage)
        h = i // 4
        m = i % 4
        left = rows[h, :, :, pl.ds(pl.multiple_of(m * 256, 256), 256)].reshape(all_rows, 256)
        for q in range(4):
            staged[i, q] = lax.dot_general(
                left, grads[:, q * units:(q + 1) * units], (((0,), (0,)), ((), ())),
                preferred_element_type=F32,
            )
        for which in range(2):
            out_local(i, which).start()
            out_remote(i, which).start()

    finish1(1)
    finish1(3)
    for h, s in both:
        reduce2(h, s, "o").start()
    relay1(0)
    for h, s in both:
        reduce2(h, s, "f").wait_recv()
        alpha, beta = along(h)
        add_into(h, block(h, shifted(alpha, SIGN[s], 4), beta), s, [(far2.at[h, s], 0)])
        reduce2(h, s, "w").start()
    finish1(0)
    for h, s in both:
        reduce2(h, s, "o").wait_recv()
        reduce2(h, s, "w").wait_recv()
    for h in (0, 1):
        for p in (0, 1):
            base = p * part_rows
            add_into(h, here, p, [(near2.at[h, 0], base), (near2.at[h, 1], base)])

    for dz, dc in peers:
        bring(dz, dc).start()
    own_out.start()

    expert_c = lax.broadcasted_iota(jnp.int32, (tokens, slots), 1)
    named = (ids_ref[:, 0:1] == expert_c // cap) | (ids_ref[:, 1:2] == expert_c // cap)
    before = (
        lax.broadcasted_iota(jnp.int32, (tokens, tokens), 1)
        < lax.broadcasted_iota(jnp.int32, (tokens, tokens), 0)
    )
    slot = jnp.dot(
        before.astype(F32).astype(BF16), named.astype(F32).astype(BF16),
        preferred_element_type=F32,
    )
    pick = jnp.where(named & (slot == (expert_c % cap).astype(F32)), 1.0, 0.0).astype(BF16)

    own_out.wait()
    for dz, dc in peers:
        bring(dz, dc).wait_recv()
    for core in range(2):
        for h in range(2):
            at = core * half + h * quarter
            tg_ref[:, at:at + quarter] = jnp.dot(
                pick, returned[core, h], preferred_element_type=F32
            ).astype(BF16)

    for dz, dc in peers:
        spread(dz, dc).wait_send()
        bring(dz, dc).wait_send()
    for which in range(2):
        weight_out(which).wait_send()
    grads_out().wait_send()
    for h, s in both:
        for t in ("f", "o", "w"):
            gather1(h, s, t).wait_send()
            reduce2(h, s, t).wait_send()
            for k in range(4):
                gather2(h, s, k, t).wait_send()
                reduce1(h, s, k, t).wait_send()

    @pl.loop(0, 8)
    def _(i):
        for which in range(2):
            out_local(i, which).wait()
            out_remote(i, which).wait()


MESSAGES = 7 + 7 + 2 + 1 + 12 + 48 + 48 + 12


def on_device(tokens, expert_ids, weight_gate, weight_up, gate_pre, up_pre, hidden_grad):
    count, width = tokens.shape
    slots, units = gate_pre.shape[1:]
    quarter = width // 4
    lines = slots // 16
    vmem = pl.BlockSpec(memory_space=pltpu.VMEM)
    anywhere = pl.BlockSpec(memory_space=pl.ANY)
    dma = pltpu.SemaphoreType.DMA
    return pl.pallas_call(
        kernel,
        out_shape=(
            jax.ShapeDtypeStruct((count, width), BF16),
            jax.ShapeDtypeStruct((1, width, units), F32),
            jax.ShapeDtypeStruct((1, width, units), F32),
        ),
        in_specs=[vmem] * 3 + [anywhere] * 5,
        out_specs=(vmem, anywhere, anywhere),
        scratch_shapes=[
            pltpu.VMEM((2, 16, lines, quarter), BF16),
            pltpu.VMEM((slots, 4 * units), BF16),
            pltpu.VMEM((2 * quarter, 4 * units), BF16),
            pltpu.VMEM((2, 16, lines, quarter), BF16),
            pltpu.VMEM((2, 2, 4, lines, quarter), BF16),
            pltpu.VMEM((2, 2, 4, lines // 2, quarter), BF16),
            pltpu.VMEM((2, 2, lines, quarter), BF16),
            pltpu.VMEM((2, 2, lines // 2, quarter), BF16),
            pltpu.VMEM((8, 4, 256, units), F32),
            pltpu.VMEM((3, slots, units), BF16),
            pltpu.VMEM((2, 2, 64, quarter), BF16),
            pltpu.VMEM((2, 2, 64, quarter), BF16),
            dma((MESSAGES,)),
            dma((MESSAGES,)),
            dma((7,)),
            dma((8, 2)),
            dma((8, 2)),
            dma((8, 2)),
        ],
        compiler_params=pltpu.CompilerParams(
            collective_id=0, has_side_effects=True, vmem_limit_bytes=60 * 1024 * 1024
        ),
    )(expert_ids, expert_ids.T, tokens, weight_gate, weight_up, gate_pre, up_pre, hidden_grad)


def solution(mesh):
    torus = Mesh(
        mesh.devices.reshape(mesh.shape["expert"], 4, 4, 2),
        ("expert", "shard_0", "shard_1", "shard_2"),
    )
    split = P("expert", None, SHARD)
    placed = (P(EXPERT_SHARD, None), P(EXPERT_SHARD, None), split, split, split, split, split)
    return jax.shard_map(
        on_device,
        mesh=torus,
        in_specs=placed,
        out_specs=(P(EXPERT_SHARD, None), split, split),
        check_vma=False,
    )
```

time: 219 us -> 125 us (0.57)
  Pallas kernels: 0 us -> 114 us
  waiting for transfers between devices: 92.8 us -> 0 us
  matrix products: 59 us -> 0 us
  local copies, waits for them, and re-layouts: 30.3 us -> 9.63 us
  between operations: 15.6 us -> 0.64 us
  blocking collectives: 14.4 us -> 0 us
  starting transfers between devices: 4.48 us -> 0 us
    pallas_call x0 -> x1, Pallas kernels: none -> 114 us  [on_device(): pl.pallas_call(kernel, out_shape=(jax.ShapeDtypeStruct((count, width), BF...]
    dot_general x6 -> x0, matrix products: 59 us -> none  [the longest x3 37.7 us: times_transposed(): lax.dot_general(left_rows, weights, (((1,), (1,)), ((), ())), preferred_e...]
    all_gather x2 -> x0, waiting for transfers between devices: 56.7 us -> none  [all_blocks(): tiles = lax.all_gather(tiles, axes[k])]
    unnamed x5 -> x0, waiting for transfers between devices: 28.3 us -> none
    all_to_all x1 -> x0, blocking collectives: 14.4 us -> none  [on_device(): lax.all_to_all(outgoing.reshape(groups, capacity, model_width), 'expert',...]
    another operation x1 -> x0, local copies, waits for them, and re-layouts: 14.1 us -> none  [scatter_pairs(): tiles = tiles.reshape(*sizes, *inside).swapaxes(0, 1).reshape(-1, *inside)]
    transpose x1 -> x0, local copies, waits for them, and re-layouts: 8.84 us -> none  [all_blocks(): tiles = tiles.transpose(*back, *range(len(axes), tiles.ndim))]
    reduce_scatter x1 -> x0, waiting for transfers between devices: 7.82 us -> none  [scatter_pairs(): tiles = lax.psum_scatter(tiles, core, scatter_dimension=0, tiled=True)]
  transfers between devices with their start and end apart: 5 -> 0, of which waited for: 4 -> 0; matrix products, arithmetic and copies ran while one was open for 36% -> 0% of each run, Pallas kernels for 0% -> 0%
where the time goes in v1:
time: 125 us; the launch traced here: 124 us
  Pallas kernels  114 us (91%)
  local copies, waits for them, and re-layouts  9.63 us (8%)
    pallas_call x1, Pallas kernels, on_device(): pl.pallas_call(kernel, out_shape=(jax.ShapeDtypeStruct((count, width), BF...  114 us
    unnamed x6, local copies, waits for them, and re-layouts  9.63 us

profile of v1, /device:TPU:1, one launch (start us, length us, event | category | flops | bytes accessed | tf_op | source)
XLA Modules:
  0.0 124.4 jit_solution(3657200250137349541)
XLA Ops:
  0.6 1.4 %copy.10.ids_ref = s32[24,2]{1,0:T(8,128)} copy(s32[24,2]{0,1:T(2,128)} %param.8) | data formatting | bytes 384 | tf_op args[1]
  2.0 114.1 %shard_map.94 = (bf16[24,4096]{1,0:T(8,128)(2,1)}, f32[1,4096,256]{2,1,0:T(8,128)}, f32[1,4096,256]{2,1,0:T(8,128)}) custom-call(s32[24,2]{1,0:T(8,128)} %copy.10.ids_ref, s32[2,24]{1,0:T(2,128)} %bitcast.1, bf16[24,4096]{1,0:T(8,128)(2,1)} %tok_ref.1, bf16[1,4096,256]{2,1,0:T(8,128)(2,1)} %wg_ref.1, bf16[1,4096,256]{2,1,0:T(8,128)(2,1)} %wu_ref.1, ...), custom_call_target="tpu_custom_call" | custom-call | tf_op jit(solution)/shard_map/pallas_call | solution.py:498
  116.1 1.6 %copy.14 = bf16[24,4096]{1,0:T(8,128)(2,1)} copy(bf16[24,4096]{1,0:T(8,128)(2,1)} %get-tuple-element.6) | data formatting | bytes 393216
  117.7 0.0 copy-start
  117.7 4.6 %copy.15 = f32[1,4096,256]{2,1,0:T(8,128)} copy(f32[1,4096,256]{2,1,0:T(8,128)} %get-tuple-element.7) | data formatting | bytes 8388608
  122.3 0.0 copy-done
  122.4 2.0 %copy.16 = f32[1,4096,256]{2,1,0:T(8,128)} copy(f32[1,4096,256]{2,1,0:T(8,128)S(1)} %copy-done) | data formatting | bytes 8388608
Async XLA Ops:
  117.7 4.6 %copy-start = (f32[1,4096,256]{2,1,0:T(8,128)S(1)}, f32[1,4096,256]{2,1,0:T(8,128)}, u32[]{:S(2)}) copy-start(f32[1,4096,256]{2,1,0:T(8,128)} %get-tuple-element.8) | copy-start | bytes 12582916

commit v2 on v1

--- a/solution.py
+++ b/solution.py
@@ -19,10 +19,48 @@
     return lax.rem(value + by % size, size)
 
 
+def picked(ids_t_ref, cap):
+    tokens = ids_t_ref.shape[1]
+    line = lax.broadcasted_iota(jnp.int32, (4 * cap, tokens), 0)
+    named = (ids_t_ref[0:1, :] == line // cap) | (ids_t_ref[1:2, :] == line // cap)
+    before = (
+        lax.broadcasted_iota(jnp.int32, (tokens, tokens), 0)
+        < lax.broadcasted_iota(jnp.int32, (tokens, tokens), 1)
+    )
+    slot = jnp.dot(
+        named.astype(F32).astype(BF16), before.astype(F32).astype(BF16), preferred_element_type=F32
+    )
+    return jnp.where(named & (slot == (line % cap).astype(F32)), 1.0, 0.0).astype(BF16)
+
+
+def finish(ids_t_ref, returned, og_in, ou_in, tg_ref, og_ref, ou_ref, sems):
+    width = og_in.shape[1] // 4
+
+    def put(i):
+        which, q = i // 4, i % 4
+        at = pl.ds(q * width, width)
+        return pltpu.make_async_copy(
+            (og_in, ou_in)[which].at[0, at, :], (og_ref, ou_ref)[which].at[0, at, :], sems.at[i]
+        )
+
+    for i in range(8):
+        put(i).start()
+    pick_t = picked(ids_t_ref, 16)
+    quarter = returned.shape[3]
+    for core in range(2):
+        for h in range(2):
+            at = (2 * core + h) * quarter
+            tg_ref[:, at:at + quarter] = lax.dot_general(
+                pick_t, returned[core, h], (((0,), (0,)), ((), ())), preferred_element_type=F32
+            ).astype(BF16)
+    for i in range(8):
+        put(i).wait()
+
+
 def kernel(
-    ids_ref, ids_t_ref, tok_ref, wg_ref, wu_ref, gate_ref, up_ref, hid_ref,
-    tg_ref, og_ref, ou_ref,
-    rows, grads, weights, terms, near1, far1, near2, far2, staged, pre, outgoing, returned,
+    ids_t_ref, tok_ref, wg_ref, wu_ref, gate_ref, up_ref, hid_ref,
+    returned, og_ref, ou_ref,
+    rows, grads, weights, terms, near1, far1, near2, far2, staged, pre, outgoing,
     send_sem, recv_sem, local_sem, out_sem, out_send, out_recv,
 ):
     z = lax.axis_index("expert")
@@ -190,20 +228,7 @@
             barrier, inc=1, device_id=first(h, s), device_id_type=pl.DeviceIdType.MESH
         )
 
-    slots = 4 * cap
-    expert_r = lax.broadcasted_iota(jnp.int32, (slots, tokens), 0)
-    named_t = (ids_t_ref[0:1, :] == expert_r // cap) | (ids_t_ref[1:2, :] == expert_r // cap)
-    before_t = (
-        lax.broadcasted_iota(jnp.int32, (tokens, tokens), 0)
-        < lax.broadcasted_iota(jnp.int32, (tokens, tokens), 1)
-    )
-    slot_t = jnp.dot(
-        named_t.astype(F32).astype(BF16), before_t.astype(F32).astype(BF16),
-        preferred_element_type=F32,
-    )
-    pick_t = jnp.where(
-        named_t & (slot_t == (expert_r % cap).astype(F32)), 1.0, 0.0
-    ).astype(BF16)
+    pick_t = picked(ids_t_ref, cap)
     for core in range(2):
         for h in range(2):
             at = core * half + h * quarter
@@ -441,28 +466,9 @@
         bring(dz, dc).start()
     own_out.start()
 
-    expert_c = lax.broadcasted_iota(jnp.int32, (tokens, slots), 1)
-    named = (ids_ref[:, 0:1] == expert_c // cap) | (ids_ref[:, 1:2] == expert_c // cap)
-    before = (
-        lax.broadcasted_iota(jnp.int32, (tokens, tokens), 1)
-        < lax.broadcasted_iota(jnp.int32, (tokens, tokens), 0)
-    )
-    slot = jnp.dot(
-        before.astype(F32).astype(BF16), named.astype(F32).astype(BF16),
-        preferred_element_type=F32,
-    )
-    pick = jnp.where(named & (slot == (expert_c % cap).astype(F32)), 1.0, 0.0).astype(BF16)
-
     own_out.wait()
     for dz, dc in peers:
         bring(dz, dc).wait_recv()
-    for core in range(2):
-        for h in range(2):
-            at = core * half + h * quarter
-            tg_ref[:, at:at + quarter] = jnp.dot(
-                pick, returned[core, h], preferred_element_type=F32
-            ).astype(BF16)
-
     for dz, dc in peers:
         spread(dz, dc).wait_send()
         bring(dz, dc).wait_send()
@@ -495,15 +501,16 @@
     vmem = pl.BlockSpec(memory_space=pltpu.VMEM)
     anywhere = pl.BlockSpec(memory_space=pl.ANY)
     dma = pltpu.SemaphoreType.DMA
-    return pl.pallas_call(
+    ids_t = expert_ids.T
+    returned, gate_out, up_out = pl.pallas_call(
         kernel,
         out_shape=(
-            jax.ShapeDtypeStruct((count, width), BF16),
-            jax.ShapeDtypeStruct((1, width, units), F32),
-            jax.ShapeDtypeStruct((1, width, units), F32),
+            pltpu.VMEM((2, 2, 64, quarter), BF16),
+            pltpu.VMEM((1, width, units), F32),
+            pltpu.VMEM((1, width, units), F32),
         ),
-        in_specs=[vmem] * 3 + [anywhere] * 5,
-        out_specs=(vmem, anywhere, anywhere),
+        in_specs=[vmem] * 2 + [anywhere] * 5,
+        out_specs=(anywhere, anywhere, anywhere),
         scratch_shapes=[
             pltpu.VMEM((2, 16, lines, quarter), BF16),
             pltpu.VMEM((slots, 4 * units), BF16),
@@ -516,7 +523,6 @@
             pltpu.VMEM((8, 4, 256, units), F32),
             pltpu.VMEM((3, slots, units), BF16),
             pltpu.VMEM((2, 2, 64, quarter), BF16),
-            pltpu.VMEM((2, 2, 64, quarter), BF16),
             dma((MESSAGES,)),
             dma((MESSAGES,)),
             dma((7,)),
@@ -525,9 +531,21 @@
             dma((8, 2)),
         ],
         compiler_params=pltpu.CompilerParams(
-            collective_id=0, has_side_effects=True, vmem_limit_bytes=60 * 1024 * 1024
+            collective_id=0, has_side_effects=True, vmem_limit_bytes=46 * 1024 * 1024
         ),
-    )(expert_ids, expert_ids.T, tokens, weight_gate, weight_up, gate_pre, up_pre, hidden_grad)
+    )(ids_t, tokens, weight_gate, weight_up, gate_pre, up_pre, hidden_grad)
+    return pl.pallas_call(
+        finish,
+        out_shape=(
+            jax.ShapeDtypeStruct((count, width), BF16),
+            jax.ShapeDtypeStruct((1, width, units), F32),
+            jax.ShapeDtypeStruct((1, width, units), F32),
+        ),
+        in_specs=[vmem, vmem, anywhere, anywhere],
+        out_specs=(vmem, anywhere, anywhere),
+        scratch_shapes=[dma((8,))],
+        compiler_params=pltpu.CompilerParams(vmem_limit_bytes=8 * 1024 * 1024),
+    )(ids_t, returned, gate_out, up_out)
 
 
 def solution(mesh):

time: 125 us -> 118 us (0.944)
  local copies, waits for them, and re-layouts: 9.63 us -> 0.01 us
  Pallas kernels: 114 us -> 117 us
    unnamed x6 -> x2, local copies, waits for them, and re-layouts: 9.63 us -> 0.01 us
    pallas_call x1 -> x2, Pallas kernels: 114 us -> 117 us  [the longest x1 113 us: on_device(): pl.pallas_call(kernel, out_shape=(pltpu.VMEM((2, 2, 64, quarter), BF16),...]
where the time goes in v2:
time: 118 us
  Pallas kernels  117 us (99%)
    pallas_call x1, Pallas kernels, on_device(): pl.pallas_call(kernel, out_shape=(pltpu.VMEM((2, 2, 64, quarter), BF16),...  113 us
    pallas_call x1, Pallas kernels, on_device(): pl.pallas_call(finish, out_shape=(jax.ShapeDtypeStruct((count, width), BF...  4.05 us

profile of v2, /device:TPU:1, one launch (start us, length us, event | category | flops | bytes accessed | tf_op | source)
XLA Modules:
  0.0 117.9 jit_solution(15966767576625230458)
XLA Ops:
  0.6 0.0 copy-start
  0.6 113.2 %shard_map.94 = (bf16[2,2,64,1024]{3,2,1,0:T(8,128)(2,1)S(1)}, f32[1,4096,256]{2,1,0:T(8,128)S(1)}, f32[1,4096,256]{2,1,0:T(8,128)S(1)}) custom-call(s32[2,24]{1,0:T(2,128)} %bitcast.1, bf16[24,4096]{1,0:T(8,128)(2,1)} %tok_ref.1, bf16[1,4096,256]{2,1,0:T(8,128)(2,1)} %wg_ref.1, bf16[1,4096,256]{2,1,0:T(8,128)(2,1)} %wu_ref.1, ...), custom_call_target="tpu_custom_call" | custom-call | tf_op jit(solution)/shard_map/pallas_call | solution.py:505
  113.9 0.0 copy-done
  113.9 4.0 %shard_map.95 = (bf16[24,4096]{1,0:T(8,128)(2,1)}, f32[1,4096,256]{2,1,0:T(8,128)}, f32[1,4096,256]{2,1,0:T(8,128)}) custom-call(s32[2,24]{1,0:T(2,128)S(1)} %bitcast.2, bf16[2,2,64,1024]{3,2,1,0:T(8,128)(2,1)S(1)} %get-tuple-element.6.returned, f32[1,4096,256]{2,1,0:T(8,128)S(1)} %get-tuple-element.7.og_in, f32[1,4096,256]{2,1,0:T(8,128)S(1)} %get-tuple-element.8.ou_in), custom_call_target="tpu_custom_call" | custom-call | tf_op jit(solution)/shard_map/pallas_call | solution.py:537
Async XLA Ops:
  0.6 113.2 %copy-start = (s32[24,2]{0,1:T(2,128)S(1)}, s32[24,2]{0,1:T(2,128)}, u32[]{:S(2)}) copy-start(s32[24,2]{0,1:T(2,128)} %param.8) | copy-start | bytes 580

commit v3 on v2

--- a/solution.py
+++ b/solution.py
@@ -19,10 +19,11 @@
     return lax.rem(value + by % size, size)
 
 
-def picked(ids_t_ref, cap):
-    tokens = ids_t_ref.shape[1]
+def picked(first_ids, second_ids, cap):
+    tokens = first_ids.shape[1]
     line = lax.broadcasted_iota(jnp.int32, (4 * cap, tokens), 0)
-    named = (ids_t_ref[0:1, :] == line // cap) | (ids_t_ref[1:2, :] == line // cap)
+    expert = (line // cap).astype(F32)
+    named = (first_ids == expert) | (second_ids == expert)
     before = (
         lax.broadcasted_iota(jnp.int32, (tokens, tokens), 0)
         < lax.broadcasted_iota(jnp.int32, (tokens, tokens), 1)
@@ -33,7 +34,7 @@
     return jnp.where(named & (slot == (line % cap).astype(F32)), 1.0, 0.0).astype(BF16)
 
 
-def finish(ids_t_ref, returned, og_in, ou_in, tg_ref, og_ref, ou_ref, sems):
+def finish(ids_t_ref, returned, summed, og_in, ou_in, tg_ref, og_ref, ou_ref, sems):
     width = og_in.shape[1] // 4
 
     def put(i):
@@ -45,22 +46,28 @@
 
     for i in range(8):
         put(i).start()
-    pick_t = picked(ids_t_ref, 16)
+    ids = ids_t_ref[...].astype(F32)
+    pick_t = picked(ids[0:1, :], ids[1:2, :], 16)
+    tokens = tg_ref.shape[0]
+    half = tg_ref.shape[1] // 2
     quarter = returned.shape[3]
     for core in range(2):
         for h in range(2):
-            at = (2 * core + h) * quarter
+            at = core * half + h * quarter
             tg_ref[:, at:at + quarter] = lax.dot_general(
                 pick_t, returned[core, h], (((0,), (0,)), ((), ())), preferred_element_type=F32
             ).astype(BF16)
+        at = core * half + 2 * quarter
+        tg_ref[:, at:(core + 1) * half] = summed[core, 0:tokens, :]
     for i in range(8):
         put(i).wait()
 
 
 def kernel(
     ids_t_ref, tok_ref, wg_ref, wu_ref, gate_ref, up_ref, hid_ref,
-    returned, og_ref, ou_ref,
-    rows, grads, weights, terms, near1, far1, near2, far2, staged, pre, outgoing,
+    returned, summed, og_ref, ou_ref,
+    rows, rows_f, grads, weights, terms, terms_f, near1, far1, near2, far2, staged, pre, outgoing,
+    block_f, plane_f, slots_f, crossed_f, totals_f, sums1_f, sums2_f, last_f,
     send_sem, recv_sem, local_sem, out_sem, out_send, out_recv,
 ):
     z = lax.axis_index("expert")
@@ -70,7 +77,8 @@
     other = 1 - c
     here = y * 4 + x
     half = tok_ref.shape[1] // 2
-    quarter = half // 2
+    quarter = rows.shape[3]
+    wide_f = rows_f.shape[5]
     units = gate_ref.shape[2]
     tokens = tok_ref.shape[0]
     cap = 16
@@ -170,6 +178,111 @@
         )
 
     partner = {"shard_2": other}
+
+    def aside1(h, o):
+        return {"shard_1": shifted(x, o, 4)} if h == 0 else {"shard_0": shifted(y, o, 4)}
+
+    def aside2(h, o):
+        return aside1(1 - h, o)
+
+    def block_out():
+        return remote(
+            ("fb",), block_f.at[other], plane_f.at[c, here * (1 - c) + (x * 4 + y) * c], partner
+        )
+
+    block_own = pltpu.make_async_copy(
+        block_f.at[c], plane_f.at[c, here * (1 - c) + (x * 4 + y) * c], local_sem.at[7]
+    )
+
+    def plane1(h, o):
+        alpha, beta = along(h)
+        ref = plane_f.at[h, beta * 4 + alpha]
+        return remote(("f1", h, o), ref, ref, aside1(h, o))
+
+    def plane2(h, o):
+        alpha, beta = along(h)
+        ref = plane_f.at[h, pl.ds(beta * 4, 4)]
+        return remote(("f2", h, o), ref, ref, aside2(h, o))
+
+    def group_rows(h, at, j):
+        return rows_f.at[at, :, 0, j] if h == 0 else rows_f.at[:, at, 1, j]
+
+    TURN = (0, 1, 3, 2)
+
+    def slots_out(h, n, dz):
+        e = shifted(z, dz, 4)
+        at = shifted(along(h)[1], TURN[n], 4)
+        return remote(
+            ("fz", h, n, dz),
+            slots_f.at[h, n, :, pl.ds(pl.multiple_of(e * cap, cap), cap), :],
+            group_rows(h, at, z),
+            {"expert": e},
+        )
+
+    def slots_own(h, n):
+        at = shifted(along(h)[1], TURN[n], 4)
+        return pltpu.make_async_copy(
+            slots_f.at[h, n, :, pl.ds(pl.multiple_of(z * cap, cap), cap), :],
+            group_rows(h, at, z),
+            local_sem.at[8 + h * 4 + n],
+        )
+
+    def picked_of(h, at):
+        ids = plane_f[h, at, tokens:tokens + 8, 0:128].astype(F32)
+        lines = plane_f.shape[2]
+        return picked(ids[0:1, 0:lines], ids[1:2, 0:lines], cap)
+
+    def make_slots(h, n):
+        at = shifted(along(h)[1], TURN[n], 4)
+
+        @pl.loop(0, 4)
+        def _(i):
+            slots_f[h, n, i] = jnp.dot(
+                picked_of(h, at * 4 + i), plane_f[h, at * 4 + i], preferred_element_type=F32
+            ).astype(BF16)
+
+        for dz in (2, 1, 3):
+            slots_out(h, n, dz).start()
+        slots_own(h, n).start()
+
+    def terms_out(g, dz):
+        j = shifted(z, dz, 4)
+        return remote(
+            ("ft", g, dz), terms_f.at[g, :, :, j], crossed_f.at[z, g], {"expert": j}
+        )
+
+    terms_own = pltpu.make_async_copy(terms_f.at[:, :, :, z], crossed_f.at[z], local_sem.at[16])
+
+    def make_totals():
+        for h in (0, 1):
+            @pl.loop(0, 16)
+            def _(i):
+                one, two = i // 4, i % 4
+                held = crossed_f[:, one, two, 0] if h == 0 else crossed_f[:, two, one, 1]
+                totals_f[h, i] = lax.dot_general(
+                    picked_of(h, i), held.reshape(4 * cap, wide_f), (((0,), (0,)), ((), ())),
+                    preferred_element_type=F32,
+                ).astype(BF16)
+
+    def back1(h, o):
+        alpha, beta = along(h)
+        return remote(
+            ("b1", h, o), totals_f.at[h, pl.ds(shifted(beta, o, 4) * 4, 4)],
+            sums1_f.at[h, o - 1], aside2(h, o),
+        )
+
+    def back2(h, o):
+        alpha, beta = along(h)
+        return remote(
+            ("b2", h, o), totals_f.at[h, beta * 4 + shifted(alpha, o, 4)],
+            sums2_f.at[h, o - 1], aside1(h, o),
+        )
+
+    def last_out():
+        return remote(("fl",), last_f.at[other], summed.at[c], partner)
+
+    last_own = pltpu.make_async_copy(last_f.at[c], summed.at[c], local_sem.at[17])
+    around = [(h, o) for o in (2, 1, 3) for h in (0, 1)]
 
     def weight_out(which):
         ref = (wg_ref, wu_ref)[which]
@@ -227,8 +340,18 @@
         pl.semaphore_signal(
             barrier, inc=1, device_id=first(h, s), device_id_type=pl.DeviceIdType.MESH
         )
-
-    pick_t = picked(ids_t_ref, cap)
+    for h in (0, 1):
+        pl.semaphore_signal(
+            barrier, inc=1, device_id=aside1(h, 2), device_id_type=pl.DeviceIdType.MESH
+        )
+
+    ids = ids_t_ref[...].astype(F32)
+    pick_t = picked(ids[0:1, :], ids[1:2, :], cap)
+    for core in range(2):
+        at = core * half + 2 * quarter
+        block_f[core, 0:tokens, :] = tok_ref[:, at:at + wide_f]
+        block_f[core, tokens:, :] = jnp.full((block_f.shape[1] - tokens, wide_f), 9.0, BF16)
+        block_f[core, tokens:tokens + 2, 0:tokens] = ids.astype(BF16)
     for core in range(2):
         for h in range(2):
             at = core * half + h * quarter
@@ -236,12 +359,19 @@
                 pick_t, tok_ref[:, at:at + quarter], preferred_element_type=F32
             ).astype(BF16)
 
-    pl.semaphore_wait(barrier, len(peers) + len(both))
+    pl.semaphore_wait(barrier, len(peers) + len(both) + 2)
+    block_out().start()
+    block_own.start()
     for dz, dc in peers:
         spread(dz, dc).start()
     own_in.start()
     for which in range(2):
         weight_out(which).start()
+
+    block_own.wait()
+    block_out().wait_recv()
+    for h, o in around:
+        plane1(h, o).start()
 
     for which in range(3):
         pre_in(which).wait()
@@ -265,6 +395,10 @@
     for t in ("f", "o"):
         for h, s in both:
             gather1(h, s, t).start()
+    for h, o in around:
+        plane1(h, o).wait_recv()
+    for h, o in around:
+        plane2(h, o).start()
     for t in ("f", "o"):
         for h, s in both:
             gather2(h, s, 0, t).start()
@@ -273,7 +407,15 @@
         for s in ((0, 1) if p == 0 else (1, 0)):
             gather2(h, s, k, "f" if s == p else "o").start()
 
+    def group_stage(n):
+        for h in (0, 1):
+            if n:
+                plane2(h, (None, 3, 1, 2)[n]).wait_recv()
+            make_slots(h, n)
+
     def gather_stage(i):
+        if i == 0:
+            group_stage(0)
         if i == 1:
             for h, s in both:
                 gather1(h, s, "f", True).wait_recv()
@@ -287,10 +429,15 @@
             for h in (0, 1):
                 send_part(h, 3, 1)
                 send_part(h, 1, 0)
+            for g in range(4):
+                for dz in (2, 1, 3):
+                    terms_out(g, dz).start()
+            terms_own.start()
         if i == 3:
             for h, s in both:
                 gather2(h, s, 0, "f", True).wait_recv()
                 gather2(h, s, 0, "w").start()
+            group_stage(1)
         if i == 4:
             for h, s in both:
                 gather1(h, s, "w", True).wait_recv()
@@ -299,11 +446,13 @@
                 gather2(h, 1, 2, "f").start()
                 gather2(h, 0, 2, "o").start()
                 gather2(h, 1, 2, "o").start()
+            group_stage(2)
         if i == 5:
             for h in (0, 1):
                 for s, k in ((0, 3), (1, 1)):
                     gather2(h, s, k, "f", True).wait_recv()
                     gather2(h, s, k, "w").start()
+            group_stage(3)
         if i == 6:
             for h in (0, 1):
                 for s, k in ((0, 1), (1, 3)):
@@ -319,23 +468,30 @@
 
     @pl.loop(0, 8)
     def _(i):
-        for stage in range(1, 7):
+        for stage in range(7):
             @pl.when(i == stage)
             def _():
                 gather_stage(stage)
-        h = i // 4
-        g = i % 4
-
-        @pl.loop(0, quarter // 256)
-        def _(n):
+        tile = (i + 6) % 8
+
+        @pl.loop(0, 4)
+        def _(g):
             left = grads[pl.ds(pl.multiple_of(g * group, group), group), :]
-            right = weights[pl.ds(pl.multiple_of(h * quarter + n * 256, 256), 256), :]
+            right = weights[pl.ds(pl.multiple_of(tile * 256, 256), 256), :]
             out = lax.dot_general(
                 left, right, (((1,), (1,)), ((), ())), preferred_element_type=F32
             ).astype(BF16)
-            terms[h, pl.ds(g * 4, 4), :, pl.ds(pl.multiple_of(n * 256, 256), 256)] = out.reshape(
-                4, rows.shape[2], 256
-            )
+
+            @pl.when(tile < 6)
+            def _():
+                terms[
+                    tile // 3, pl.ds(g * 4, 4), :, pl.ds(pl.multiple_of(tile % 3 * 256, 256), 256)
+                ] = out.reshape(4, rows.shape[2], 256)
+
+            for m in range(2):
+                @pl.when(tile == 6 + m)
+                def _():
+                    terms_f[g, :, :, :, :, m * 256:(m + 1) * 256] = out.reshape(4, 2, 4, cap, 256)
 
     for h, s in both:
         gather2(h, s, 2, "f", True).wait_recv()
@@ -431,17 +587,42 @@
             @pl.when(i == stage)
             def _():
                 reduce_stage(stage)
-        h = i // 4
-        m = i % 4
-        left = rows[h, :, :, pl.ds(pl.multiple_of(m * 256, 256), 256)].reshape(all_rows, 256)
-        for q in range(4):
-            staged[i, q] = lax.dot_general(
-                left, grads[:, q * units:(q + 1) * units], (((0,), (0,)), ((), ())),
-                preferred_element_type=F32,
-            )
+        def multiply(left):
+            for q in range(4):
+                staged[i, q] = lax.dot_general(
+                    left, grads[:, q * units:(q + 1) * units], (((0,), (0,)), ((), ())),
+                    preferred_element_type=F32,
+                )
+
+        @pl.when(i < 6)
+        def _():
+            at = pl.ds(pl.multiple_of(i % 3 * 256, 256), 256)
+            multiply(rows[i // 3, :, :, at].reshape(all_rows, 256))
+
+        @pl.when(i == 6)
+        def _():
+            for h in (0, 1):
+                for n in range(4):
+                    for dz in (2, 1, 3):
+                        slots_out(h, n, dz).wait_recv()
+                    slots_own(h, n).wait()
+
+        @pl.when(i >= 6)
+        def _():
+            at = pl.ds(pl.multiple_of((i - 6) % 2 * 256, 256), 256)
+            multiply(rows_f[:, :, :, :, :, at].reshape(all_rows, 256))
+
         for which in range(2):
             out_local(i, which).start()
             out_remote(i, which).start()
+
+    terms_own.wait()
+    for g in range(4):
+        for dz in (2, 1, 3):
+            terms_out(g, dz).wait_recv()
+    make_totals()
+    for h, o in around:
+        back1(h, o).start()
 
     finish1(1)
     finish1(3)
@@ -453,6 +634,20 @@
         alpha, beta = along(h)
         add_into(h, block(h, shifted(alpha, SIGN[s], 4), beta), s, [(far2.at[h, s], 0)])
         reduce2(h, s, "w").start()
+    for h in (0, 1):
+        for o in (1, 2, 3):
+            back1(h, o).wait_recv()
+        base = along(h)[1] * 4
+
+        @pl.loop(0, 4)
+        def _(i):
+            total = totals_f[h, base + i].astype(F32)
+            for o in range(3):
+                total = total + sums1_f[h, o, i].astype(F32)
+            totals_f[h, base + i] = total.astype(BF16)
+
+        for o in (2, 1, 3):
+            back2(h, o).start()
     finish1(0)
     for h, s in both:
         reduce2(h, s, "o").wait_recv()
@@ -466,6 +661,18 @@
         bring(dz, dc).start()
     own_out.start()
 
+    for h in (0, 1):
+        for o in (1, 2, 3):
+            back2(h, o).wait_recv()
+        alpha, beta = along(h)
+        total = totals_f[h, beta * 4 + alpha].astype(F32)
+        for o in range(3):
+            total = total + sums2_f[h, o].astype(F32)
+        last_f[h] = total.astype(BF16)
+    last_out().start()
+    last_own.start()
+    last_own.wait()
+    last_out().wait_recv()
     own_out.wait()
     for dz, dc in peers:
         bring(dz, dc).wait_recv()
@@ -475,6 +682,20 @@
     for which in range(2):
         weight_out(which).wait_send()
     grads_out().wait_send()
+    block_out().wait_send()
+    last_out().wait_send()
+    for h, o in around:
+        plane1(h, o).wait_send()
+        plane2(h, o).wait_send()
+        back1(h, o).wait_send()
+        back2(h, o).wait_send()
+    for h in (0, 1):
+        for n in range(4):
+            for dz in (2, 1, 3):
+                slots_out(h, n, dz).wait_send()
+    for g in range(4):
+        for dz in (2, 1, 3):
+            terms_out(g, dz).wait_send()
     for h, s in both:
         for t in ("f", "o", "w"):
             gather1(h, s, t).wait_send()
@@ -490,32 +711,36 @@
             out_remote(i, which).wait()
 
 
-MESSAGES = 7 + 7 + 2 + 1 + 12 + 48 + 48 + 12
+MESSAGES = 7 + 7 + 2 + 1 + 12 + 48 + 48 + 12 + 1 + 1 + 4 * 6 + 24 + 12
 
 
 def on_device(tokens, expert_ids, weight_gate, weight_up, gate_pre, up_pre, hidden_grad):
     count, width = tokens.shape
     slots, units = gate_pre.shape[1:]
-    quarter = width // 4
+    wide_f = width // 8
+    quarter = (width // 2 - wide_f) // 2
     lines = slots // 16
     vmem = pl.BlockSpec(memory_space=pltpu.VMEM)
     anywhere = pl.BlockSpec(memory_space=pl.ANY)
     dma = pltpu.SemaphoreType.DMA
     ids_t = expert_ids.T
-    returned, gate_out, up_out = pl.pallas_call(
+    returned, summed, gate_out, up_out = pl.pallas_call(
         kernel,
         out_shape=(
             pltpu.VMEM((2, 2, 64, quarter), BF16),
+            pltpu.VMEM((2, 32, wide_f), BF16),
             pltpu.VMEM((1, width, units), F32),
             pltpu.VMEM((1, width, units), F32),
         ),
         in_specs=[vmem] * 2 + [anywhere] * 5,
-        out_specs=(anywhere, anywhere, anywhere),
+        out_specs=(anywhere,) * 4,
         scratch_shapes=[
             pltpu.VMEM((2, 16, lines, quarter), BF16),
+            pltpu.VMEM((4, 4, 2, 4, 16, wide_f), BF16),
             pltpu.VMEM((slots, 4 * units), BF16),
-            pltpu.VMEM((2 * quarter, 4 * units), BF16),
+            pltpu.VMEM((width // 2, 4 * units), BF16),
             pltpu.VMEM((2, 16, lines, quarter), BF16),
+            pltpu.VMEM((4, 4, 2, 4, 16, wide_f), BF16),
             pltpu.VMEM((2, 2, 4, lines, quarter), BF16),
             pltpu.VMEM((2, 2, 4, lines // 2, quarter), BF16),
             pltpu.VMEM((2, 2, lines, quarter), BF16),
@@ -523,15 +748,23 @@
             pltpu.VMEM((8, 4, 256, units), F32),
             pltpu.VMEM((3, slots, units), BF16),
             pltpu.VMEM((2, 2, 64, quarter), BF16),
+            pltpu.VMEM((2, 32, wide_f), BF16),
+            pltpu.VMEM((2, 16, 32, wide_f), BF16),
+            pltpu.VMEM((2, 4, 4, 64, wide_f), BF16),
+            pltpu.VMEM((4, 4, 4, 2, 16, wide_f), BF16),
+            pltpu.VMEM((2, 16, 32, wide_f), BF16),
+            pltpu.VMEM((2, 3, 4, 32, wide_f), BF16),
+            pltpu.VMEM((2, 3, 32, wide_f), BF16),
+            pltpu.VMEM((2, 32, wide_f), BF16),
             dma((MESSAGES,)),
             dma((MESSAGES,)),
-            dma((7,)),
+            dma((18,)),
             dma((8, 2)),
             dma((8, 2)),
             dma((8, 2)),
         ],
         compiler_params=pltpu.CompilerParams(
-            collective_id=0, has_side_effects=True, vmem_limit_bytes=46 * 1024 * 1024
+            collective_id=0, has_side_effects=True, vmem_limit_bytes=51 * 1024 * 1024
         ),
     )(ids_t, tokens, weight_gate, weight_up, gate_pre, up_pre, hidden_grad)
     return pl.pallas_call(
@@ -541,11 +774,11 @@
             jax.ShapeDtypeStruct((1, width, units), F32),
             jax.ShapeDtypeStruct((1, width, units), F32),
         ),
-        in_specs=[vmem, vmem, anywhere, anywhere],
+        in_specs=[vmem, vmem, vmem, anywhere, anywhere],
         out_specs=(vmem, anywhere, anywhere),
         scratch_shapes=[dma((8,))],
         compiler_params=pltpu.CompilerParams(vmem_limit_bytes=8 * 1024 * 1024),
-    )(ids_t, returned, gate_out, up_out)
+    )(ids_t, returned, summed, gate_out, up_out)
 
 
 def solution(mesh):

time: 118 us -> 111 us (0.941)
  Pallas kernels: 117 us -> 110 us
    pallas_call x1, Pallas kernels: 113 us -> 106 us  [on_device(): pl.pallas_call(kernel, out_shape=(pltpu.VMEM((2, 2, 64, quarter), BF16),...]
where the time goes in v3:
time: 111 us
  Pallas kernels  110 us (99%)
    pallas_call x1, Pallas kernels, on_device(): pl.pallas_call(kernel, out_shape=(pltpu.VMEM((2, 2, 64, quarter), BF16),...  106 us
    pallas_call x1, Pallas kernels, on_device(): pl.pallas_call(finish, out_shape=(jax.ShapeDtypeStruct((count, width), BF...  4.07 us

profile of v3, /device:TPU:1, one launch (start us, length us, event | category | flops | bytes accessed | tf_op | source)
XLA Modules:
  0.0 111.0 jit_solution(8491059104256190457)
XLA Ops:
  0.6 0.0 copy-start
  0.6 106.2 %shard_map.94 = (bf16[2,2,64,768]{3,2,1,0:T(8,128)(2,1)S(1)}, bf16[2,32,512]{2,1,0:T(8,128)(2,1)S(1)}, f32[1,4096,256]{2,1,0:T(8,128)S(1)}, f32[1,4096,256]{2,1,0:T(8,128)S(1)}) custom-call(s32[2,24]{1,0:T(2,128)} %bitcast.1, bf16[24,4096]{1,0:T(8,128)(2,1)} %tok_ref.1, bf16[1,4096,256]{2,1,0:T(8,128)(2,1)} %wg_ref.1, bf16[1,4096,256]{2,1,0:T(8,128)(2,1)} %wu_ref.1, ...), custom_call_target="tpu_custom_call" | custom-call | tf_op jit(solution)/shard_map/pallas_call | solution.py:727
  106.9 0.0 copy-done
  106.9 4.1 %shard_map.95 = (bf16[24,4096]{1,0:T(8,128)(2,1)}, f32[1,4096,256]{2,1,0:T(8,128)}, f32[1,4096,256]{2,1,0:T(8,128)}) custom-call(s32[2,24]{1,0:T(2,128)S(1)} %bitcast.2, bf16[2,2,64,768]{3,2,1,0:T(8,128)(2,1)S(1)} %get-tuple-element.7.returned, bf16[2,32,512]{2,1,0:T(8,128)(2,1)S(1)} %get-tuple-element.8.summed, f32[1,4096,256]{2,1,0:T(8,128)S(1)} %get-tuple-element.9.og_in, ...), custom_call_target="tpu_custom_call" | custom-call | tf_op jit(solution)/shard_map/pallas_call | solution.py:770
Async XLA Ops:
  0.6 106.3 %copy-start = (s32[24,2]{0,1:T(2,128)S(1)}, s32[24,2]{0,1:T(2,128)}, u32[]{:S(2)}) copy-start(s32[24,2]{0,1:T(2,128)} %param.8) | copy-start | bytes 580

commit v4 on v3

--- a/solution.py
+++ b/solution.py
@@ -58,7 +58,7 @@
                 pick_t, returned[core, h], (((0,), (0,)), ((), ())), preferred_element_type=F32
             ).astype(BF16)
         at = core * half + 2 * quarter
-        tg_ref[:, at:(core + 1) * half] = summed[core, 0:tokens, :]
+        tg_ref[:, at:(core + 1) * half] = summed[core]
     for i in range(8):
         put(i).wait()
 
@@ -260,8 +260,8 @@
                 one, two = i // 4, i % 4
                 held = crossed_f[:, one, two, 0] if h == 0 else crossed_f[:, two, one, 1]
                 totals_f[h, i] = lax.dot_general(
-                    picked_of(h, i), held.reshape(4 * cap, wide_f), (((0,), (0,)), ((), ())),
-                    preferred_element_type=F32,
+                    picked_of(h, i)[:, 0:tokens], held.reshape(4 * cap, wide_f),
+                    (((0,), (0,)), ((), ())), preferred_element_type=F32,
                 ).astype(BF16)
 
     def back1(h, o):
@@ -365,19 +365,20 @@
     for dz, dc in peers:
         spread(dz, dc).start()
     own_in.start()
-    for which in range(2):
-        weight_out(which).start()
-
     block_own.wait()
     block_out().wait_recv()
     for h, o in around:
         plane1(h, o).start()
 
+    for which in range(2):
+        weight_out(which).start()
+
     for which in range(3):
         pre_in(which).wait()
 
-    @pl.loop(0, pre.shape[1] // 64)
-    def _(i):
+    pieces = pre.shape[1] // 64
+
+    def make_grads(i):
         at = pl.ds(pl.multiple_of(i * 64, 64), 64)
         a = pre[0, at, :].astype(F32)
         b = pre[1, at, :].astype(F32)
@@ -387,6 +388,12 @@
         grads[at, 0:units] = (gs * b * (1.0 + a * (1.0 - sig))).astype(BF16)
         grads[at, units:2 * units] = (gs * a).astype(BF16)
 
+    pl.loop(0, pieces // 2)(make_grads)
+    for h, o in around:
+        plane1(h, o).wait_recv()
+    for h, o in around:
+        plane2(h, o).start()
+    pl.loop(pieces // 2, pieces)(make_grads)
     grads_out().start()
 
     own_in.wait()
@@ -395,10 +402,6 @@
     for t in ("f", "o"):
         for h, s in both:
             gather1(h, s, t).start()
-    for h, o in around:
-        plane1(h, o).wait_recv()
-    for h, o in around:
-        plane2(h, o).start()
     for t in ("f", "o"):
         for h, s in both:
             gather2(h, s, 0, t).start()
@@ -559,6 +562,26 @@
             for h, s in both:
                 reduce2(h, s, "f").start()
             send1(0, "o")
+        if i == 5:
+            terms_own.wait()
+            for g in range(4):
+                for dz in (2, 1, 3):
+                    terms_out(g, dz).wait_recv()
+            make_totals()
+        if i == 6:
+            finish1(1)
+            finish1(3)
+            for h, s in both:
+                reduce2(h, s, "o").start()
+            relay1(0)
+        if i == 7:
+            for h, s in both:
+                reduce2(h, s, "f").wait_recv()
+                alpha, beta = along(h)
+                add_into(h, block(h, shifted(alpha, SIGN[s], 4), beta), s, [(far2.at[h, s], 0)])
+                reduce2(h, s, "w").start()
+            for h, o in around:
+                back1(h, o).start()
 
     def out_rows(i):
         at = pl.multiple_of(c * half + i * 256, 256)
@@ -583,7 +606,7 @@
 
     @pl.loop(0, 8)
     def _(i):
-        for stage in range(1, 5):
+        for stage in range(1, 8):
             @pl.when(i == stage)
             def _():
                 reduce_stage(stage)
@@ -616,38 +639,6 @@
             out_local(i, which).start()
             out_remote(i, which).start()
 
-    terms_own.wait()
-    for g in range(4):
-        for dz in (2, 1, 3):
-            terms_out(g, dz).wait_recv()
-    make_totals()
-    for h, o in around:
-        back1(h, o).start()
-
-    finish1(1)
-    finish1(3)
-    for h, s in both:
-        reduce2(h, s, "o").start()
-    relay1(0)
-    for h, s in both:
-        reduce2(h, s, "f").wait_recv()
-        alpha, beta = along(h)
-        add_into(h, block(h, shifted(alpha, SIGN[s], 4), beta), s, [(far2.at[h, s], 0)])
-        reduce2(h, s, "w").start()
-    for h in (0, 1):
-        for o in (1, 2, 3):
-            back1(h, o).wait_recv()
-        base = along(h)[1] * 4
-
-        @pl.loop(0, 4)
-        def _(i):
-            total = totals_f[h, base + i].astype(F32)
-            for o in range(3):
-                total = total + sums1_f[h, o, i].astype(F32)
-            totals_f[h, base + i] = total.astype(BF16)
-
-        for o in (2, 1, 3):
-            back2(h, o).start()
     finish1(0)
     for h, s in both:
         reduce2(h, s, "o").wait_recv()
@@ -660,6 +651,22 @@
     for dz, dc in peers:
         bring(dz, dc).start()
     own_out.start()
+
+    for h in (0, 1):
+        for o in (1, 2, 3):
+            back1(h, o).wait_recv()
+        base = along(h)[1] * 4
+
+        @pl.loop(0, 4)
+        def _(i):
+            total = totals_f[h, base + i].astype(F32)
+            for o in range(3):
+                total = total + sums1_f[h, o, i].astype(F32)
+            totals_f[h, base + i] = total.astype(BF16)
+
+        for o in (2, 1, 3):
+            back2(h, o).start()
+
 
     for h in (0, 1):
         for o in (1, 2, 3):
@@ -728,7 +735,7 @@
         kernel,
         out_shape=(
             pltpu.VMEM((2, 2, 64, quarter), BF16),
-            pltpu.VMEM((2, 32, wide_f), BF16),
+            pltpu.VMEM((2, count, wide_f), BF16),
             pltpu.VMEM((1, width, units), F32),
             pltpu.VMEM((1, width, units), F32),
         ),
@@ -752,10 +759,10 @@
             pltpu.VMEM((2, 16, 32, wide_f), BF16),
             pltpu.VMEM((2, 4, 4, 64, wide_f), BF16),
             pltpu.VMEM((4, 4, 4, 2, 16, wide_f), BF16),
-            pltpu.VMEM((2, 16, 32, wide_f), BF16),
-            pltpu.VMEM((2, 3, 4, 32, wide_f), BF16),
-            pltpu.VMEM((2, 3, 32, wide_f), BF16),
-            pltpu.VMEM((2, 32, wide_f), BF16),
+            pltpu.VMEM((2, 16, count, wide_f), BF16),
+            pltpu.VMEM((2, 3, 4, count, wide_f), BF16),
+            pltpu.VMEM((2, 3, count, wide_f), BF16),
+            pltpu.VMEM((2, count, wide_f), BF16),
             dma((MESSAGES,)),
             dma((MESSAGES,)),
             dma((18,)),

time: 111 us -> 104 us (0.937)
  Pallas kernels: 110 us -> 103 us
    pallas_call x1, Pallas kernels: 106 us -> 99 us  [on_device(): pl.pallas_call(kernel, out_shape=(pltpu.VMEM((2, 2, 64, quarter), BF16),...]
where the time goes in v4:
time: 104 us
  Pallas kernels  103 us (99%)
    pallas_call x1, Pallas kernels, on_device(): pl.pallas_call(kernel, out_shape=(pltpu.VMEM((2, 2, 64, quarter), BF16),...  99 us
    pallas_call x1, Pallas kernels, on_device(): pl.pallas_call(finish, out_shape=(jax.ShapeDtypeStruct((count, width), BF...  4.07 us

profile of v4, /device:TPU:1, one launch (start us, length us, event | category | flops | bytes accessed | tf_op | source)
XLA Modules:
  0.0 103.8 jit_solution(8903065302686306578)
XLA Ops:
  0.6 0.0 copy-start
  0.6 99.0 %shard_map.94 = (bf16[2,2,64,768]{3,2,1,0:T(8,128)(2,1)S(1)}, bf16[2,24,512]{2,1,0:T(8,128)(2,1)S(1)}, f32[1,4096,256]{2,1,0:T(8,128)S(1)}, f32[1,4096,256]{2,1,0:T(8,128)S(1)}) custom-call(s32[2,24]{1,0:T(2,128)} %bitcast.1, bf16[24,4096]{1,0:T(8,128)(2,1)} %tok_ref.1, bf16[1,4096,256]{2,1,0:T(8,128)(2,1)} %wg_ref.1, bf16[1,4096,256]{2,1,0:T(8,128)(2,1)} %wu_ref.1, ...), custom_call_target="tpu_custom_call" | custom-call | tf_op jit(solution)/shard_map/pallas_call | solution.py:734
  99.7 0.0 copy-done
  99.7 4.1 %shard_map.95 = (bf16[24,4096]{1,0:T(8,128)(2,1)}, f32[1,4096,256]{2,1,0:T(8,128)}, f32[1,4096,256]{2,1,0:T(8,128)}) custom-call(s32[2,24]{1,0:T(2,128)S(1)} %bitcast.2, bf16[2,2,64,768]{3,2,1,0:T(8,128)(2,1)S(1)} %get-tuple-element.7.returned, bf16[2,24,512]{2,1,0:T(8,128)(2,1)S(1)} %get-tuple-element.8.summed, f32[1,4096,256]{2,1,0:T(8,128)S(1)} %get-tuple-element.9.og_in, ...), custom_call_target="tpu_custom_call" | custom-call | tf_op jit(solution)/shard_map/pallas_call | solution.py:777
Async XLA Ops:
  0.6 99.1 %copy-start = (s32[24,2]{0,1:T(2,128)S(1)}, s32[24,2]{0,1:T(2,128)}, u32[]{:S(2)}) copy-start(s32[24,2]{0,1:T(2,128)} %param.8) | copy-start | bytes 580

commit v5 on v4

--- a/solution.py
+++ b/solution.py
@@ -34,7 +34,7 @@
     return jnp.where(named & (slot == (line % cap).astype(F32)), 1.0, 0.0).astype(BF16)
 
 
-def finish(ids_t_ref, returned, summed, og_in, ou_in, tg_ref, og_ref, ou_ref, sems):
+def finish(ids_t_ref, returned, summed, og_in, ou_in, tg_out, og_ref, ou_ref, tg_ref, sems):
     width = og_in.shape[1] // 4
 
     def put(i):
@@ -59,15 +59,36 @@
             ).astype(BF16)
         at = core * half + 2 * quarter
         tg_ref[:, at:(core + 1) * half] = summed[core]
+    tg_copy = pltpu.make_async_copy(tg_ref, tg_out, sems.at[8])
+    tg_copy.start()
     for i in range(8):
         put(i).wait()
+    tg_copy.wait()
+
+
+class Together:
+    def __init__(self, *copies):
+        self.copies = copies
+
+    def start(self):
+        for copy in self.copies:
+            copy.start()
+
+    def wait_recv(self):
+        for copy in self.copies:
+            copy.wait_recv()
+
+    def wait_send(self):
+        for copy in self.copies:
+            copy.wait_send()
 
 
 def kernel(
-    ids_t_ref, tok_ref, wg_ref, wu_ref, gate_ref, up_ref, hid_ref,
+    ids_any, tok_any, wg_ref, wu_ref, gate_ref, up_ref, hid_ref,
     returned, summed, og_ref, ou_ref,
     rows, rows_f, grads, weights, terms, terms_f, near1, far1, near2, far2, staged, pre, outgoing,
     block_f, plane_f, slots_f, crossed_f, totals_f, sums1_f, sums2_f, last_f,
+    ids_t_ref, tok_ref, block_ids, plane_ids,
     send_sem, recv_sem, local_sem, out_sem, out_send, out_recv,
 ):
     z = lax.axis_index("expert")
@@ -186,23 +207,35 @@
         return aside1(1 - h, o)
 
     def block_out():
-        return remote(
-            ("fb",), block_f.at[other], plane_f.at[c, here * (1 - c) + (x * 4 + y) * c], partner
+        at = here * (1 - c) + (x * 4 + y) * c
+        return Together(
+            remote(("ib",), block_ids, plane_ids.at[c, at], partner),
+            remote(("fb",), block_f.at[other], plane_f.at[c, at], partner),
         )
 
     block_own = pltpu.make_async_copy(
         block_f.at[c], plane_f.at[c, here * (1 - c) + (x * 4 + y) * c], local_sem.at[7]
     )
 
+    ids_own = pltpu.make_async_copy(
+        block_ids, plane_ids.at[c, here * (1 - c) + (x * 4 + y) * c], local_sem.at[20]
+    )
+
     def plane1(h, o):
         alpha, beta = along(h)
-        ref = plane_f.at[h, beta * 4 + alpha]
-        return remote(("f1", h, o), ref, ref, aside1(h, o))
+        ids, ref = plane_ids.at[h, beta * 4 + alpha], plane_f.at[h, beta * 4 + alpha]
+        return Together(
+            remote(("i1", h, o), ids, ids, aside1(h, o)),
+            remote(("f1", h, o), ref, ref, aside1(h, o)),
+        )
 
     def plane2(h, o):
         alpha, beta = along(h)
-        ref = plane_f.at[h, pl.ds(beta * 4, 4)]
-        return remote(("f2", h, o), ref, ref, aside2(h, o))
+        ids, ref = plane_ids.at[h, pl.ds(beta * 4, 4)], plane_f.at[h, pl.ds(beta * 4, 4)]
+        return Together(
+            remote(("i2", h, o), ids, ids, aside2(h, o)),
+            remote(("f2", h, o), ref, ref, aside2(h, o)),
+        )
 
     def group_rows(h, at, j):
         return rows_f.at[at, :, 0, j] if h == 0 else rows_f.at[:, at, 1, j]
@@ -228,9 +261,8 @@
         )
 
     def picked_of(h, at):
-        ids = plane_f[h, at, tokens:tokens + 8, 0:128].astype(F32)
-        lines = plane_f.shape[2]
-        return picked(ids[0:1, 0:lines], ids[1:2, 0:lines], cap)
+        ids = plane_ids[h, at].astype(F32)
+        return picked(ids[0:1, 0:tokens], ids[1:2, 0:tokens], cap)
 
     def make_slots(h, n):
         at = shifted(along(h)[1], TURN[n], 4)
@@ -260,7 +292,7 @@
                 one, two = i // 4, i % 4
                 held = crossed_f[:, one, two, 0] if h == 0 else crossed_f[:, two, one, 1]
                 totals_f[h, i] = lax.dot_general(
-                    picked_of(h, i)[:, 0:tokens], held.reshape(4 * cap, wide_f),
+                    picked_of(h, i), held.reshape(4 * cap, wide_f),
                     (((0,), (0,)), ((), ())), preferred_element_type=F32,
                 ).astype(BF16)
 
@@ -325,6 +357,10 @@
     peers = [(dz, dc) for dz in (2, 1, 3, 0) for dc in (0, 1) if (dz, dc) != (0, 0)]
     both = [(h, s) for h in (0, 1) for s in (0, 1)]
 
+    ids_in = pltpu.make_async_copy(ids_any, ids_t_ref, local_sem.at[18])
+    tok_in = pltpu.make_async_copy(tok_any, tok_ref, local_sem.at[19])
+    ids_in.start()
+    tok_in.start()
     for which in range(3):
         pre_in(which).start()
     for which in range(2):
@@ -345,13 +381,15 @@
             barrier, inc=1, device_id=aside1(h, 2), device_id_type=pl.DeviceIdType.MESH
         )
 
+    ids_in.wait()
+    tok_in.wait()
     ids = ids_t_ref[...].astype(F32)
     pick_t = picked(ids[0:1, :], ids[1:2, :], cap)
     for core in range(2):
         at = core * half + 2 * quarter
-        block_f[core, 0:tokens, :] = tok_ref[:, at:at + wide_f]
-        block_f[core, tokens:, :] = jnp.full((block_f.shape[1] - tokens, wide_f), 9.0, BF16)
-        block_f[core, tokens:tokens + 2, 0:tokens] = ids.astype(BF16)
+        block_f[core] = tok_ref[:, at:at + wide_f]
+    block_ids[...] = jnp.zeros(block_ids.shape, BF16)
+    block_ids[0:2, 0:tokens] = ids.astype(BF16)
     for core in range(2):
         for h in range(2):
             at = core * half + h * quarter
@@ -362,10 +400,12 @@
     pl.semaphore_wait(barrier, len(peers) + len(both) + 2)
     block_out().start()
     block_own.start()
+    ids_own.start()
     for dz, dc in peers:
         spread(dz, dc).start()
     own_in.start()
     block_own.wait()
+    ids_own.wait()
     block_out().wait_recv()
     for h, o in around:
         plane1(h, o).start()
@@ -718,7 +758,7 @@
             out_remote(i, which).wait()
 
 
-MESSAGES = 7 + 7 + 2 + 1 + 12 + 48 + 48 + 12 + 1 + 1 + 4 * 6 + 24 + 12
+MESSAGES = 7 + 7 + 2 + 1 + 12 + 48 + 48 + 12 + 1 + 1 + 4 * 6 + 24 + 12 + 13
 
 
 def on_device(tokens, expert_ids, weight_gate, weight_up, gate_pre, up_pre, hidden_grad):
@@ -739,7 +779,7 @@
             pltpu.VMEM((1, width, units), F32),
             pltpu.VMEM((1, width, units), F32),
         ),
-        in_specs=[vmem] * 2 + [anywhere] * 5,
+        in_specs=[anywhere] * 7,
         out_specs=(anywhere,) * 4,
         scratch_shapes=[
             pltpu.VMEM((2, 16, lines, quarter), BF16),
@@ -755,17 +795,21 @@
             pltpu.VMEM((8, 4, 256, units), F32),
             pltpu.VMEM((3, slots, units), BF16),
             pltpu.VMEM((2, 2, 64, quarter), BF16),
-            pltpu.VMEM((2, 32, wide_f), BF16),
-            pltpu.VMEM((2, 16, 32, wide_f), BF16),
+            pltpu.VMEM((2, count, wide_f), BF16),
+            pltpu.VMEM((2, 16, count, wide_f), BF16),
             pltpu.VMEM((2, 4, 4, 64, wide_f), BF16),
             pltpu.VMEM((4, 4, 4, 2, 16, wide_f), BF16),
             pltpu.VMEM((2, 16, count, wide_f), BF16),
             pltpu.VMEM((2, 3, 4, count, wide_f), BF16),
             pltpu.VMEM((2, 3, count, wide_f), BF16),
             pltpu.VMEM((2, count, wide_f), BF16),
+            pltpu.VMEM(expert_ids.shape[::-1], jnp.int32),
+            pltpu.VMEM((count, width), BF16),
+            pltpu.VMEM((8, 128), BF16),
+            pltpu.VMEM((2, 16, 8, 128), BF16),
             dma((MESSAGES,)),
             dma((MESSAGES,)),
-            dma((18,)),
+            dma((21,)),
             dma((8, 2)),
             dma((8, 2)),
             dma((8, 2)),
@@ -782,8 +826,8 @@
             jax.ShapeDtypeStruct((1, width, units), F32),
         ),
         in_specs=[vmem, vmem, vmem, anywhere, anywhere],
-        out_specs=(vmem, anywhere, anywhere),
-        scratch_shapes=[dma((8,))],
+        out_specs=(anywhere,) * 3,
+        scratch_shapes=[pltpu.VMEM((count, width), BF16), dma((9,))],
         compiler_params=pltpu.CompilerParams(vmem_limit_bytes=8 * 1024 * 1024),
     )(ids_t, returned, summed, gate_out, up_out)
 

time: 104 us -> 101 us (0.971)
  Pallas kernels: 103 us -> 101 us
    pallas_call x1, Pallas kernels: 99 us -> 97.2 us  [on_device(): pl.pallas_call(kernel, out_shape=(pltpu.VMEM((2, 2, 64, quarter), BF16),...]
where the time goes in v5:
time: 101 us
  Pallas kernels  101 us (100%)
    pallas_call x1, Pallas kernels, on_device(): pl.pallas_call(kernel, out_shape=(pltpu.VMEM((2, 2, 64, quarter), BF16),...  97.2 us
    pallas_call x1, Pallas kernels, on_device(): pl.pallas_call(finish, out_shape=(jax.ShapeDtypeStruct((count, width), BF...  3.4 us

profile of v5, /device:TPU:1, one launch (start us, length us, event | category | flops | bytes accessed | tf_op | source)
XLA Modules:
  0.0 101.3 jit_solution(1253814933909161537)
XLA Ops:
  0.6 0.0 copy-start
  0.6 97.2 %shard_map.94 = (bf16[2,2,64,768]{3,2,1,0:T(8,128)(2,1)S(1)}, bf16[2,24,512]{2,1,0:T(8,128)(2,1)S(1)}, f32[1,4096,256]{2,1,0:T(8,128)S(1)}, f32[1,4096,256]{2,1,0:T(8,128)S(1)}) custom-call(s32[2,24]{1,0:T(2,128)} %bitcast.1, bf16[24,4096]{1,0:T(8,128)(2,1)} %tok_any.1, bf16[1,4096,256]{2,1,0:T(8,128)(2,1)} %wg_ref.1, bf16[1,4096,256]{2,1,0:T(8,128)(2,1)} %wu_ref.1, ...), custom_call_target="tpu_custom_call" | custom-call | tf_op jit(solution)/shard_map/pallas_call | solution.py:774
  97.8 0.0 copy-done
  97.9 3.4 %shard_map.95 = (bf16[24,4096]{1,0:T(8,128)(2,1)}, f32[1,4096,256]{2,1,0:T(8,128)}, f32[1,4096,256]{2,1,0:T(8,128)}) custom-call(s32[2,24]{1,0:T(2,128)S(1)} %bitcast.2, bf16[2,2,64,768]{3,2,1,0:T(8,128)(2,1)S(1)} %get-tuple-element.7.returned, bf16[2,24,512]{2,1,0:T(8,128)(2,1)S(1)} %get-tuple-element.8.summed, f32[1,4096,256]{2,1,0:T(8,128)S(1)} %get-tuple-element.9.og_in, ...), custom_call_target="tpu_custom_call" | custom-call | tf_op jit(solution)/shard_map/pallas_call | solution.py:821
Async XLA Ops:
  0.6 97.2 %copy-start = (s32[24,2]{0,1:T(2,128)S(1)}, s32[24,2]{0,1:T(2,128)}, u32[]{:S(2)}) copy-start(s32[24,2]{0,1:T(2,128)} %param.8) | copy-start | bytes 580

commit v6 on v5

--- a/solution.py
+++ b/solution.py
@@ -136,21 +136,42 @@
     def part(p):
         return pl.ds(p * part_rows, part_rows)
 
-    def gather1(h, s, t, arriving=False):
+    def quarter_of(p, dz):
+        if dz is None:
+            return part(p)
+        return pl.ds(pl.multiple_of(p * part_rows + shifted(z, dz, 4) * cap, cap), cap)
+
+    def gather1(h, s, t, arriving=False, dz=None):
         alpha, beta = along(h)
         back = (1 if t == "w" else 0) + (1 if arriving else 0)
         p = 1 - s if t == "o" else s
-        ref = rows.at[h, block(h, shifted(alpha, -SIGN[s] * back, 4), beta), part(p)]
-        return remote(("a1", h, s, t), ref, ref, first(h, s))
-
-    def gather2(h, s, k, t, arriving=False):
+        at = block(h, shifted(alpha, -SIGN[s] * back, 4), beta)
+        ref = rows.at[h, at, quarter_of(p, dz)]
+        return remote(("a1", h, s, t, dz), ref, ref, first(h, s))
+
+    def gather2(h, s, k, t, arriving=False, dz=None):
         alpha, beta = along(h)
         back = (1 if t == "w" else 0) + (1 if arriving else 0)
         p = 1 - s if t == "o" else s
-        ref = rows.at[
-            h, block(h, shifted(alpha, k, 4), shifted(beta, -SIGN[s] * back, 4)), part(p)
-        ]
-        return remote(("a2", h, s, k, t), ref, ref, second(h, s))
+        at = block(h, shifted(alpha, k, 4), shifted(beta, -SIGN[s] * back, 4))
+        ref = rows.at[h, at, quarter_of(p, dz)]
+        return remote(("a2", h, s, k, t, dz), ref, ref, second(h, s))
+
+    def send_own(dz):
+        for t in ("f", "o"):
+            for h, s in both:
+                gather1(h, s, t, dz=dz).start()
+        for t in ("f", "o"):
+            for h, s in both:
+                gather2(h, s, 0, t, dz=dz).start()
+
+    def got1(h, s, t):
+        for dz in range(4):
+            gather1(h, s, t, True, dz).wait_recv()
+
+    def got2(h, s, t):
+        for dz in range(4):
+            gather2(h, s, 0, t, True, dz).wait_recv()
 
     def reduce1(h, s, k, t):
         alpha, beta = along(h)
@@ -354,7 +375,7 @@
         local_sem.at[6],
     )
 
-    peers = [(dz, dc) for dz in (2, 1, 3, 0) for dc in (0, 1) if (dz, dc) != (0, 0)]
+    peers = [(0, 1)] + [(dz, dc) for dz in (2, 1, 3) for dc in (0, 1)]
     both = [(h, s) for h in (0, 1) for s in (0, 1)]
 
     ids_in = pltpu.make_async_copy(ids_any, ids_t_ref, local_sem.at[18])
@@ -409,7 +430,9 @@
     block_out().wait_recv()
     for h, o in around:
         plane1(h, o).start()
-
+    own_in.wait()
+    spread(0, 1).wait_recv()
+    send_own(0)
     for which in range(2):
         weight_out(which).start()
 
@@ -433,18 +456,13 @@
         plane1(h, o).wait_recv()
     for h, o in around:
         plane2(h, o).start()
+    for dz in (1, 3, 2):
+        for dc in (0, 1):
+            spread(dz, dc).wait_recv()
+        send_own(4 - dz)
+
     pl.loop(pieces // 2, pieces)(make_grads)
     grads_out().start()
-
-    own_in.wait()
-    for dz, dc in peers:
-        spread(dz, dc).wait_recv()
-    for t in ("f", "o"):
-        for h, s in both:
-            gather1(h, s, t).start()
-    for t in ("f", "o"):
-        for h, s in both:
-            gather2(h, s, 0, t).start()
 
     def send_part(h, k, p):
         for s in ((0, 1) if p == 0 else (1, 0)):
@@ -461,14 +479,14 @@
             group_stage(0)
         if i == 1:
             for h, s in both:
-                gather1(h, s, "f", True).wait_recv()
+                got1(h, s, "f")
                 gather1(h, s, "w").start()
             for h in (0, 1):
                 send_part(h, 3, 0)
                 send_part(h, 1, 1)
         if i == 2:
             for h, s in both:
-                gather1(h, s, "o", True).wait_recv()
+                got1(h, s, "o")
             for h in (0, 1):
                 send_part(h, 3, 1)
                 send_part(h, 1, 0)
@@ -478,7 +496,7 @@
             terms_own.start()
         if i == 3:
             for h, s in both:
-                gather2(h, s, 0, "f", True).wait_recv()
+                got2(h, s, "f")
                 gather2(h, s, 0, "w").start()
             group_stage(1)
         if i == 4:
@@ -546,7 +564,10 @@
 
     for h, s in both:
         for k in (0, 1, 3, 2):
-            gather2(h, s, k, "o", True).wait_recv()
+            if k:
+                gather2(h, s, k, "o", True).wait_recv()
+            else:
+                got2(h, s, "o")
             gather2(h, s, k, "w", True).wait_recv()
 
     def add_into(h, at, p, sources):
@@ -613,6 +634,8 @@
             finish1(3)
             for h, s in both:
                 reduce2(h, s, "o").start()
+            for h, o in around[0:2]:
+                back1(h, o).start()
             relay1(0)
         if i == 7:
             for h, s in both:
@@ -620,7 +643,7 @@
                 alpha, beta = along(h)
                 add_into(h, block(h, shifted(alpha, SIGN[s], 4), beta), s, [(far2.at[h, s], 0)])
                 reduce2(h, s, "w").start()
-            for h, o in around:
+            for h, o in around[2:]:
                 back1(h, o).start()
 
     def out_rows(i):
@@ -745,10 +768,13 @@
             terms_out(g, dz).wait_send()
     for h, s in both:
         for t in ("f", "o", "w"):
-            gather1(h, s, t).wait_send()
+            for dz in (None,) if t == "w" else range(4):
+                gather1(h, s, t, dz=dz).wait_send()
+                gather2(h, s, 0, t, dz=dz).wait_send()
             reduce2(h, s, t).wait_send()
             for k in range(4):
-                gather2(h, s, k, t).wait_send()
+                if k:
+                    gather2(h, s, k, t).wait_send()
                 reduce1(h, s, k, t).wait_send()
 
     @pl.loop(0, 8)
@@ -758,7 +784,7 @@
             out_remote(i, which).wait()
 
 
-MESSAGES = 7 + 7 + 2 + 1 + 12 + 48 + 48 + 12 + 1 + 1 + 4 * 6 + 24 + 12 + 13
+MESSAGES = 7 + 7 + 2 + 1 + 12 + 48 + 48 + 12 + 48 + 1 + 1 + 4 * 6 + 24 + 12 + 13
 
 
 def on_device(tokens, expert_ids, weight_gate, weight_up, gate_pre, up_pre, hidden_grad):

time: 101 us -> 101 us (level)
  no operation moved by 1% of the time
where the time goes in v6:
time: 101 us
  Pallas kernels  100 us (99%)
    pallas_call x1, Pallas kernels, on_device(): pl.pallas_call(kernel, out_shape=(pltpu.VMEM((2, 2, 64, quarter), BF16),...  96.9 us
    pallas_call x1, Pallas kernels, on_device(): pl.pallas_call(finish, out_shape=(jax.ShapeDtypeStruct((count, width), BF...  3.4 us

profile of v6, /device:TPU:1, one launch (start us, length us, event | category | flops | bytes accessed | tf_op | source)
XLA Modules:
  0.0 101.0 jit_solution(12591345239656004857)
XLA Ops:
  0.6 0.0 copy-start
  0.6 96.9 %shard_map.94 = (bf16[2,2,64,768]{3,2,1,0:T(8,128)(2,1)S(1)}, bf16[2,24,512]{2,1,0:T(8,128)(2,1)S(1)}, f32[1,4096,256]{2,1,0:T(8,128)S(1)}, f32[1,4096,256]{2,1,0:T(8,128)S(1)}) custom-call(s32[2,24]{1,0:T(2,128)} %bitcast.1, bf16[24,4096]{1,0:T(8,128)(2,1)} %tok_any.1, bf16[1,4096,256]{2,1,0:T(8,128)(2,1)} %wg_ref.1, bf16[1,4096,256]{2,1,0:T(8,128)(2,1)} %wu_ref.1, ...), custom_call_target="tpu_custom_call" | custom-call | tf_op jit(solution)/shard_map/pallas_call | solution.py:800
  97.6 0.0 copy-done
  97.6 3.4 %shard_map.95 = (bf16[24,4096]{1,0:T(8,128)(2,1)}, f32[1,4096,256]{2,1,0:T(8,128)}, f32[1,4096,256]{2,1,0:T(8,128)}) custom-call(s32[2,24]{1,0:T(2,128)S(1)} %bitcast.2, bf16[2,2,64,768]{3,2,1,0:T(8,128)(2,1)S(1)} %get-tuple-element.7.returned, bf16[2,24,512]{2,1,0:T(8,128)(2,1)S(1)} %get-tuple-element.8.summed, f32[1,4096,256]{2,1,0:T(8,128)S(1)} %get-tuple-element.9.og_in, ...), custom_call_target="tpu_custom_call" | custom-call | tf_op jit(solution)/shard_map/pallas_call | solution.py:847
Async XLA Ops:
  0.6 97.0 %copy-start = (s32[24,2]{0,1:T(2,128)S(1)}, s32[24,2]{0,1:T(2,128)}, u32[]{:S(2)}) copy-start(s32[24,2]{0,1:T(2,128)} %param.8) | copy-start | bytes 580
